TPU v7x, 32 devices: a whole 2x2x4 slice. The times are simulated.
32 devices in a mesh: gx: 2 (over x), gy: 4 (over y, core), gz: 4 (over z).
Axes of the slice: x: 2, y: 2, z: 4, core: 2. Of those that a mesh axis runs over, the one named last changes fastest.
Arguments:
- conserved: float32 [5, 16, 32, 256], P(None, 'gz', 'gy', 'gx'), may hold values from -3 to 12, as said below
- metrics: float32 [9, 16, 32, 256], P(None, 'gz', 'gy', 'gx'), may hold values from -0.6 to 2, as said below
- inv_volume: float32 [16, 32, 256], P('gz', 'gy', 'gx'), may hold values from 0.5 to 2
- wake_donor: int32 [256], P('gx'), may hold values from -1 to 255, as said below
Outputs:
- section_state: float32 [5, 16, 32, 256], P(None, 'gz', 'gy', 'gx')
- time_rate: float32 [5, 16, 32, 256], P(None, 'gz', 'gy', 'gx')
Inputs may be any that keep to these rules, and one draw needn't show every extreme that they name: `conserved`: each cell holds density rho of 0.5 to 2, pressure p of 0.5 to 2 and velocity components u of -1.5 to 1.5 as (rho, rho u, p / 0.4 + rho |u|^2 / 2). `metrics`: in each cell, row d (entries 3 d to 3 d + 2) has its entry 3 d + d between 0.5 and 2 and its other two entries at most 0.3 times that entry in magnitude. wake_donor[i] is either 256 - 1 - i or -1, and wake_donor[i] >= 0 exactly where wake_donor[255 - i] >= 0.
All inputs are finite; a program needn't handle non-finite values.
Results may differ from a plain program's by a relative error of at most 0.0001.
Values sent between devices are 32-bit elements; how exact they have to be, the bound alone decides.
A program may use at most 64 MiB of HBM per device.

v0:
```python
import jax
import jax.numpy as jnp
from jax import lax
from jax.sharding import PartitionSpec as P

GAMMA = 1.4
WENO_EPS = 1e-06
STEP_SIZE = 0.08


def padded(block, sides, width, periodic):
    for axis, dim in sides:
        count = lax.axis_size(axis)
        forward = [(i, i + 1) for i in range(count - 1)]
        if periodic:
            forward.append((count - 1, 0))
        backward = [(target, source) for source, target in forward]
        low = lax.ppermute(
            lax.slice_in_dim(block, block.shape[dim] - width, None, axis=dim), axis, forward
        )
        high = lax.ppermute(lax.slice_in_dim(block, 0, width, axis=dim), axis, backward)
        block = jnp.concatenate([low, block, high], axis=dim)
    return block


def slab_of(values, start, amount, axis):
    return lax.slice_in_dim(values, start, start + amount, axis=values.ndim + axis)


def cross_of(first, second):
    return [
        first[1] * second[2] - first[2] * second[1],
        first[2] * second[0] - first[0] * second[2],
        first[0] * second[1] - first[1] * second[0],
    ]


def inner_of(first, second):
    return first[0] * second[0] + first[1] * second[1] + first[2] * second[2]


def cell_terms(fields, metric_row):
    density = fields[0]
    velocity = fields[1:4] / density
    kinetic = 0.5 * jnp.sum(fields[1:4] * velocity, axis=0)
    pressure = (GAMMA - 1.0) * (fields[4] - kinetic)
    contra = jnp.sum(metric_row * velocity, axis=0)
    fluxes = jnp.stack(
        [
            fields[0] * contra,
            fields[1] * contra + metric_row[0] * pressure,
            fields[2] * contra + metric_row[1] * pressure,
            fields[3] * contra + metric_row[2] * pressure,
            (fields[4] + pressure) * contra,
        ]
    )
    sound_speed = jnp.sqrt(GAMMA * pressure / density)
    speeds = jnp.abs(contra) + sound_speed * jnp.sqrt(jnp.sum(metric_row * metric_row, axis=0))
    primitive = jnp.concatenate([density[None], velocity, pressure[None]], axis=0)
    return (primitive, fluxes, speeds)


def eigen_pair(state, metric_row, pick):
    density = state[0]
    velocity = [state[1], state[2], state[3]]
    pressure = state[4]
    row_size = jnp.sqrt(metric_row[0] ** 2 + metric_row[1] ** 2 + metric_row[2] ** 2)
    normal = [metric_row[member] / row_size for member in range(3)]
    axis_unit = [1.0 if member == pick else 0.0 for member in range(3)]
    raw_cross = cross_of(normal, axis_unit)
    raw_size = jnp.sqrt(raw_cross[0] ** 2 + raw_cross[1] ** 2 + raw_cross[2] ** 2)
    tangent = [raw_cross[member] / raw_size for member in range(3)]
    binormal = cross_of(normal, tangent)
    sound_speed = jnp.sqrt(GAMMA * pressure / density)
    inverse = 1.0 / sound_speed
    kinetic = 0.5 * inner_of(velocity, velocity)
    enthalpy = GAMMA / (GAMMA - 1.0) * pressure / density + kinetic
    normal_speed = inner_of(normal, velocity)
    tangent_speed = inner_of(tangent, velocity)
    binormal_speed = inner_of(binormal, velocity)
    factor = (GAMMA - 1.0) * inverse * inverse
    scaled = factor * kinetic
    left_rows = [
        [0.5 * (scaled + normal_speed * inverse)]
        + [0.5 * (-factor * velocity[member] - normal[member] * inverse) for member in range(3)]
        + [0.5 * factor],
        [1.0 - scaled] + [factor * velocity[member] for member in range(3)] + [-factor],
        [-tangent_speed] + tangent + [0.0],
        [-binormal_speed] + binormal + [0.0],
        [0.5 * (scaled - normal_speed * inverse)]
        + [0.5 * (-factor * velocity[member] + normal[member] * inverse) for member in range(3)]
        + [0.5 * factor],
    ]
    right_columns = [
        [1.0]
        + [velocity[member] - sound_speed * normal[member] for member in range(3)]
        + [enthalpy - sound_speed * normal_speed],
        [1.0] + velocity + [kinetic],
        [0.0] + tangent + [tangent_speed],
        [0.0] + binormal + [binormal_speed],
        [1.0]
        + [velocity[member] + sound_speed * normal[member] for member in range(3)]
        + [enthalpy + sound_speed * normal_speed],
    ]
    return (left_rows, right_columns)


def project_left(matrix, vector):
    return jnp.stack(
        [
            sum((matrix[member][second] * vector[second] for second in range(5)))
            for member in range(5)
        ]
    )


def apply_right(matrix, vector):
    return jnp.stack(
        [
            sum((matrix[second][member] * vector[second] for second in range(5)))
            for member in range(5)
        ]
    )


def weno_side(stencil):
    far_left, near_left, center, near_right, far_right = stencil
    guess_zero = (2.0 * far_left - 7.0 * near_left + 11.0 * center) / 6.0
    guess_one = (-near_left + 5.0 * center + 2.0 * near_right) / 6.0
    guess_two = (2.0 * center + 5.0 * near_right - far_right) / 6.0
    smooth_zero = (
        13.0 / 12.0 * (far_left - 2.0 * near_left + center) ** 2
        + 0.25 * (far_left - 4.0 * near_left + 3.0 * center) ** 2
    )
    smooth_one = (
        13.0 / 12.0 * (near_left - 2.0 * center + near_right) ** 2
        + 0.25 * (near_left - near_right) ** 2
    )
    smooth_two = (
        13.0 / 12.0 * (center - 2.0 * near_right + far_right) ** 2
        + 0.25 * (3.0 * center - 4.0 * near_right + far_right) ** 2
    )
    weight_zero = 0.1 / (WENO_EPS + smooth_zero) ** 2
    weight_one = 0.6 / (WENO_EPS + smooth_one) ** 2
    weight_two = 0.3 / (WENO_EPS + smooth_two) ** 2
    return (weight_zero * guess_zero + weight_one * guess_one + weight_two * guess_two) / (
        weight_zero + weight_one + weight_two
    )


def interface_flux(fields, metric_row, axis, pick):
    primitive, fluxes, speeds = cell_terms(fields, metric_row)
    faces_count = fields.shape[fields.ndim + axis] - 5
    mean_state = 0.5 * (
        slab_of(primitive, 2, faces_count, axis) + slab_of(primitive, 3, faces_count, axis)
    )
    mean_row = 0.5 * (
        slab_of(metric_row, 2, faces_count, axis) + slab_of(metric_row, 3, faces_count, axis)
    )
    left_rows, right_columns = eigen_pair(mean_state, mean_row, pick)
    max_speed = slab_of(speeds, 0, faces_count, axis)
    for offset in range(1, 6):
        max_speed = jnp.maximum(max_speed, slab_of(speeds, offset, faces_count, axis))
    upwind = []
    downwind = []
    for offset in range(6):
        state_chars = project_left(left_rows, slab_of(fields, offset, faces_count, axis))
        flux_chars = project_left(left_rows, slab_of(fluxes, offset, faces_count, axis))
        upwind.append(0.5 * (flux_chars + max_speed * state_chars))
        downwind.append(0.5 * (flux_chars - max_speed * state_chars))
    combined = weno_side(upwind[0:5]) + weno_side(downwind[5:0:-1])
    return apply_right(right_columns, combined)


def divergence(fields, metric_row, axis, pick):
    face_flux = interface_flux(fields, metric_row, axis, pick)
    cells_count = face_flux.shape[face_flux.ndim + axis] - 1
    return slab_of(face_flux, 1, cells_count, axis) - slab_of(face_flux, 0, cells_count, axis)


def fix_ends(extended, at_start, at_end):
    interior = extended[..., 3:-3]
    lower_ghost = jnp.where(at_start, jnp.repeat(interior[..., :1], 3, axis=-1), extended[..., :3])
    upper_ghost = jnp.where(at_end, jnp.repeat(interior[..., -1:], 3, axis=-1), extended[..., -3:])
    return jnp.concatenate([lower_ghost, interior, upper_ghost], axis=-1)


def fix_wall(extended, ghosts, at_start, at_end):
    interior = extended[:, :, 3:-3, :]
    lower_ghost = jnp.where(at_start, ghosts, extended[:, :, :3, :])
    upper_ghost = jnp.where(
        at_end, jnp.repeat(interior[:, :, -1:, :], 3, axis=2), extended[:, :, -3:, :]
    )
    return jnp.concatenate([lower_ghost, interior, upper_ghost], axis=2)


def local(conserved, metrics, inv_volume, wake_donor):
    at_inflow = lax.axis_index("gx") == 0
    at_outflow = lax.axis_index("gx") == lax.axis_size("gx") - 1
    at_wall = lax.axis_index("gy") == 0
    at_top = lax.axis_index("gy") == lax.axis_size("gy") - 1
    mirrored = jnp.concatenate([conserved[:, :, 2::-1, :], metrics[3:6, :, 2::-1, :]], axis=0)
    count = lax.axis_size("gx")
    mirrored = lax.ppermute(mirrored, "gx", [(i, count - 1 - i) for i in range(count)])
    mirrored = mirrored[..., ::-1]
    stream = padded(jnp.concatenate([conserved, metrics[0:3]], axis=0), (("gx", 3),), 3, False)
    normal = padded(jnp.concatenate([conserved, metrics[3:6]], axis=0), (("gy", 2),), 3, False)
    span = padded(jnp.concatenate([conserved, metrics[6:9]], axis=0), (("gz", 1),), 3, True)
    stream_flow, stream_row = stream[0:5], stream[5:8]
    normal_flow, normal_row = normal[0:5], normal[5:8]
    span_flow, span_row = span[0:5], span[5:8]
    stream_flow = fix_ends(stream_flow, at_inflow, at_outflow)
    stream_row = fix_ends(stream_row, at_inflow, at_outflow)
    momentum_sign = jnp.array([1.0, -1.0, -1.0, -1.0, 1.0], dtype=jnp.float32)[:, None, None, None]
    is_wake = wake_donor >= 0
    wake_flow = jnp.where(is_wake, mirrored[0:5], conserved[:, :, 2::-1, :] * momentum_sign)
    wake_row = jnp.where(is_wake, mirrored[5:8], metrics[3:6, :, 2::-1, :])
    normal_flow = fix_wall(normal_flow, wake_flow, at_wall, at_top)
    normal_row = fix_wall(normal_row, wake_row, at_wall, at_top)
    summed = divergence(stream_flow, stream_row, -1, 1)
    summed = summed + divergence(normal_flow, normal_row, -2, 2)
    summed = summed + divergence(span_flow, span_row, -3, 0)
    time_rate = -inv_volume[None] * summed
    return (conserved + STEP_SIZE * time_rate, time_rate)


def solution(mesh):
    placed = (P(None, "gz", "gy", "gx"), P(None, "gz", "gy", "gx"), P("gz", "gy", "gx"), P("gx"))
    return jax.shard_map(
        local,
        mesh=mesh,
        in_specs=placed,
        out_specs=(P(None, "gz", "gy", "gx"), P(None, "gz", "gy", "gx")),
        check_vma=False,
    )
```

profile of v0, /device:TPU:1, one launch (start us, length us, event | category | flops | bytes accessed | tf_op | source)
XLA Modules:
  0.0 32.6 jit_solution(12134740979248576491)
XLA Ops:
  0.6 0.9 %fusion.193 = (f32[3,4,8,128]{3,2,1,0:T(8,128)S(1)}, f32[3,4,8,128]{3,2,1,0:T(8,128)S(1)}, f32[3,4,8,128]{3,2,1,0:T(8,128)S(1)}) fusion(f32[9,4,8,128]{3,2,1,0:T(8,128)} %param.6), kind=kLoop, calls=%fused_computation.683 | loop fusion | bytes 294912 | tf_op jit(solution)/shard_map/slice | solution.py:206
  1.6 1.3 %collective-permute-start.1 = (f32[8,4,8,3]{3,2,1,0:T(8,128)S(1)}, f32[8,4,8,3]{3,2,1,0:T(8,128)S(1)}, u32[]{:S(2)}, u32[]{:S(2)}) collective-permute-start(f32[8,4,8,3]{3,2,1,0:T(8,128)S(1)} %get-tuple-element.341), channel_id=1, source_target_pairs={{16,0},{17,1},{18,2},{19,3},{20,4},{21,5},{22,6},{23,7},{24,8},{25... | collective-permute-start | bytes 9224 | tf_op jit(solution)/shard_map/ppermute | solution.py:21
  2.9 4.0 %collective-permute-start = (f32[8,4,8,3]{3,2,1,0:T(8,128)S(1)}, f32[8,4,8,3]{3,2,1,0:T(8,128)S(1)}, u32[]{:S(2)}, u32[]{:S(2)}) collective-permute-start(f32[8,4,8,3]{3,2,1,0:T(8,128)S(1)} %get-tuple-element.342), channel_id=1, source_target_pairs={{0,16},{1,17},{2,18},{3,19},{4,20},{5,21},{6,22},{7,23},{8,24},{9,... | collective-permute-start | bytes 9224 | tf_op jit(solution)/shard_map/ppermute | solution.py:18
  7.0 5.2 %collective-permute-start.3 = (f32[8,4,3,128]{3,2,1,0:T(4,128)S(1)}, f32[8,4,3,128]{3,2,1,0:T(4,128)S(1)}, u32[]{:S(2)}, u32[]{:S(2)}) collective-permute-start(f32[8,4,3,128]{3,2,1,0:T(4,128)S(1)} %get-tuple-element.352), channel_id=1, source_target_pairs={{0,4},{4,8},{8,12},{1,5},{5,9},{9,13},{2,6},{6,10},{10,14},{3,7},{... | collective-permute-start | bytes 147464 | tf_op jit(solution)/shard_map/ppermute | solution.py:18
  12.3 0.7 %slice-done = f32[5,4,3,128]{3,2,1,0:T(4,128)S(1)} async-done(((f32[5,4,8,128]{3,2,1,0:T(8,128)}), f32[5,4,3,128]{3,2,1,0:T(4,128)S(1)}, s32[]{:S(2)}) %slice-start) | async-done | bytes 30744 | tf_op jit(solution)/shard_map/slice | solution.py:202
  13.2 1.9 %collective-permute-start.4 = (f32[8,4,3,128]{3,2,1,0:T(4,128)S(1)}, f32[8,4,3,128]{3,2,1,0:T(4,128)S(1)}, u32[]{:S(2)}, u32[]{:S(2)}) collective-permute-start(f32[8,4,3,128]{3,2,1,0:T(4,128)S(1)} %get-tuple-element.351), channel_id=1, source_target_pairs={{4,0},{8,4},{12,8},{5,1},{9,5},{13,9},{6,2},{10,6},{14,10},{7,3},{... | collective-permute-start | bytes 147464 | tf_op jit(solution)/shard_map/ppermute | solution.py:21
  15.1 0.2 slice_reduce_fusion.1
  15.4 0.2 slice_reduce_fusion.3
  15.6 0.7 %copy-done.3 = f32[4,8,128]{2,1,0:T(8,128)S(1)} copy-done((f32[4,8,128]{2,1,0:T(8,128)S(1)}, f32[4,8,128]{2,1,0:T(8,128)}, u32[]{:S(2)}) %copy-start.3) | copy-done | bytes 16408
  16.3 1.3 %collective-permute-start.5 = (f32[8,3,8,128]{3,2,1,0:T(8,128)S(1)}, f32[8,3,8,128]{3,2,1,0:T(8,128)S(1)}, u32[]{:S(2)}, u32[]{:S(2)}) collective-permute-start(f32[8,3,8,128]{3,2,1,0:T(8,128)S(1)} %get-tuple-element.356), channel_id=1, source_target_pairs={{0,1},{1,2},{2,3},{3,0},{4,5},{5,6},{6,7},{7,4},{8,9},{9,10},{10,1... | collective-permute-start | bytes 294920 | tf_op jit(solution)/shard_map/ppermute | solution.py:18
  17.7 2.1 %collective-permute-start.6 = (f32[8,3,8,128]{3,2,1,0:T(8,128)S(1)}, f32[8,3,8,128]{3,2,1,0:T(8,128)S(1)}, u32[]{:S(2)}, u32[]{:S(2)}) collective-permute-start(f32[8,3,8,128]{3,2,1,0:T(8,128)S(1)} %get-tuple-element.355), channel_id=1, source_target_pairs={{1,0},{2,1},{3,2},{0,3},{5,4},{6,5},{7,6},{4,7},{9,8},{10,9},{11,1... | collective-permute-start | bytes 294920 | tf_op jit(solution)/shard_map/ppermute | solution.py:21
  22.7 0.2 constant_dynamic-update-slice_fusion.43
  22.9 0.2 constant_dynamic-update-slice_fusion.52
  23.5 0.2 constant_dynamic-update-slice_fusion.41
  23.6 0.2 constant_dynamic-update-slice_fusion.40
  23.8 0.2 constant_dynamic-update-slice_fusion.23
  23.9 0.2 constant_dynamic-update-slice_fusion.22
  24.1 0.2 constant_dynamic-update-slice_fusion.21
  24.3 0.2 constant_dynamic-update-slice_fusion.20
  24.4 0.8 %divide_add_fusion.1 = f32[5,4,8,129]{3,2,1,0:T(8,128)S(1)} fusion(f32[5,4,8,129]{3,2,1,0:T(8,128)S(1)} %get-tuple-element.218, f32[5,4,8,129]{3,2,1,0:T(8,128)S(1)} %get-tuple-element.217, f32[5,4,8,129]{3,2,1,0:T(8,128)S(1)} %get-tuple-element.212, f32[5,4,8,129]{3,2,1,0:T(8,128)S(1)} %get-tuple-element.211, f32[5,4,8,129]{3,2,1,0:T(8,128)S(1)} %get-tuple-element.206, ...), kind=kLoop, calls=%fused_computation.329 | loop fusion | flops 3034080 | bytes 1089792 | tf_op jit(solution)/shard_map/add | solution.py:171
  25.6 0.5 %copy-done.4 = f32[5]{0:T(128)S(1)} copy-done((f32[5]{0:T(128)S(1)}, f32[5]{0:T(128)}, u32[]{:S(2)}) %copy-start.4) | copy-done | bytes 44
  28.6 0.8 %divide_add_fusion = f32[5,4,9,128]{3,2,1,0:T(8,128)S(1)} fusion(f32[5,4,9,128]{3,2,1,0:T(8,128)S(1)} %get-tuple-element.239, f32[5,4,9,128]{3,2,1,0:T(8,128)S(1)} %get-tuple-element.238, f32[5,4,9,128]{3,2,1,0:T(8,128)S(1)} %get-tuple-element.233, f32[5,4,9,128]{3,2,1,0:T(8,128)S(1)} %get-tuple-element.232, f32[5,4,9,128]{3,2,1,0:T(8,128)S(1)} %get-tuple-element.227, ...), kind=kLoop, calls=%fused_computation.322 | loop fusion | flops 3386880 | bytes 1216512 | tf_op jit(solution)/shard_map/add | solution.py:171
  31.1 0.5 %divide_add_fusion.2 = f32[5,5,8,128]{3,2,1,0:T(8,128)S(1)} fusion(f32[5,5,8,128]{3,2,1,0:T(8,128)S(1)} %get-tuple-element.269, f32[5,5,8,128]{3,2,1,0:T(8,128)S(1)} %get-tuple-element.268, f32[5,5,8,128]{3,2,1,0:T(8,128)S(1)} %get-tuple-element.263, f32[5,5,8,128]{3,2,1,0:T(8,128)S(1)} %get-tuple-element.262, f32[5,5,8,128]{3,2,1,0:T(8,128)S(1)} %get-tuple-element.257, ...), kind=kLoop, calls=%fused_computation.346 | loop fusion | flops 3763200 | bytes 1351680 | tf_op jit(solution)/shard_map/add | solution.py:171
  31.8 0.8 %multiply_add_fusion = (f32[5,4,8,128]{3,2,1,0:T(8,128)}, f32[5,4,8,128]{3,2,1,0:T(8,128)}) fusion(f32[5,4,8,128]{3,2,1,0:T(8,128)S(1)} %copy-done.1, f32[5,5,8,128]{3,2,1,0:T(8,128)S(1)} %constant_dynamic-update-slice_fusion.190, f32[5,4,9,128]{3,2,1,0:T(8,128)S(1)} %constant_dynamic-update-slice_fusion.125, ...), kind=kLoop, calls=%fused_computation.381 | loop fusion | flops 163840 | bytes 753664 | tf_op jit(solution)/shard_map/add | solution.py:224
  (189 shorter events, 7.7 us)
Async XLA Ops:
  0.6 0.9 %copy-start = (f32[5,4,8,128]{3,2,1,0:T(8,128)S(1)}, f32[5,4,8,128]{3,2,1,0:T(8,128)}, u32[]{:S(2)}) copy-start(f32[5,4,8,128]{3,2,1,0:T(8,128)} %param.5) | copy-start | bytes 245764
  1.6 14.7 %collective-permute-start.1 = (f32[8,4,8,3]{3,2,1,0:T(8,128)S(1)}, f32[8,4,8,3]{3,2,1,0:T(8,128)S(1)}, u32[]{:S(2)}, u32[]{:S(2)}) collective-permute-start(f32[8,4,8,3]{3,2,1,0:T(8,128)S(1)} %get-tuple-element.341), channel_id=1, source_target_pairs={{16,0},{17,1},{18,2},{19,3},{20,4},{21,5},{22,6},{23,7},{24,8},{25... | collective-permute-start | bytes 9224 | tf_op jit(solution)/shard_map/ppermute | solution.py:21
  2.9 14.7 %collective-permute-start = (f32[8,4,8,3]{3,2,1,0:T(8,128)S(1)}, f32[8,4,8,3]{3,2,1,0:T(8,128)S(1)}, u32[]{:S(2)}, u32[]{:S(2)}) collective-permute-start(f32[8,4,8,3]{3,2,1,0:T(8,128)S(1)} %get-tuple-element.342), channel_id=1, source_target_pairs={{0,16},{1,17},{2,18},{3,19},{4,20},{5,21},{6,22},{7,23},{8,24},{9,... | collective-permute-start | bytes 9224 | tf_op jit(solution)/shard_map/ppermute | solution.py:18
  6.9 5.3 %copy-start.2 = (f32[9,4,8,128]{3,2,1,0:T(8,128)S(1)}, f32[9,4,8,128]{3,2,1,0:T(8,128)}, u32[]{:S(2)}) copy-start(f32[9,4,8,128]{3,2,1,0:T(8,128)} %param.6) | copy-start | bytes 442372
  7.0 18.6 %collective-permute-start.3 = (f32[8,4,3,128]{3,2,1,0:T(4,128)S(1)}, f32[8,4,3,128]{3,2,1,0:T(4,128)S(1)}, u32[]{:S(2)}, u32[]{:S(2)}) collective-permute-start(f32[8,4,3,128]{3,2,1,0:T(4,128)S(1)} %get-tuple-element.352), channel_id=1, source_target_pairs={{0,4},{4,8},{8,12},{1,5},{5,9},{9,13},{2,6},{6,10},{10,14},{3,7},{... | collective-permute-start | bytes 147464 | tf_op jit(solution)/shard_map/ppermute | solution.py:18
  12.2 0.8 %slice-start = ((f32[5,4,8,128]{3,2,1,0:T(8,128)}), f32[5,4,3,128]{3,2,1,0:T(4,128)S(1)}, s32[]{:S(2)}) async-start(f32[5,4,8,128]{3,2,1,0:T(8,128)} %param.5), calls=%async_computation | async-start | bytes 81920 | tf_op jit(solution)/shard_map/slice | solution.py:202
  13.0 2.1 %copy-start.1 = (f32[5,4,8,128]{3,2,1,0:T(8,128)S(1)}, f32[5,4,8,128]{3,2,1,0:T(8,128)}, u32[]{:S(2)}) copy-start(f32[5,4,8,128]{3,2,1,0:T(8,128)} %param.5) | copy-start | bytes 245764
  13.1 12.4 %collective-permute-start.2 = (f32[8,4,3,128]{3,2,1,0:T(4,128)S(1)}, f32[8,4,3,128]{3,2,1,0:T(4,128)S(1)}, u32[]{:S(2)}, u32[]{:S(2)}) collective-permute-start(f32[8,4,3,128]{3,2,1,0:T(4,128)S(1)} %pad_maximum_fusion.16), channel_id=1, source_target_pairs={{0,16},{16,0},{1,17},{17,1},{2,18},{18,2},{3,19},{19,3},{4,20},{20... | collective-permute-start | bytes 147464 | tf_op jit(solution)/shard_map/ppermute | solution.py:204
  13.2 2.1 %copy-start.5 = (s32[128]{0:T(128)S(1)}, s32[128]{0:T(128)}, u32[]{:S(2)}) copy-start(s32[128]{0:T(128)} %param.8) | copy-start | bytes 1540
  13.2 12.2 %collective-permute-start.4 = (f32[8,4,3,128]{3,2,1,0:T(4,128)S(1)}, f32[8,4,3,128]{3,2,1,0:T(4,128)S(1)}, u32[]{:S(2)}, u32[]{:S(2)}) collective-permute-start(f32[8,4,3,128]{3,2,1,0:T(4,128)S(1)} %get-tuple-element.351), channel_id=1, source_target_pairs={{4,0},{8,4},{12,8},{5,1},{9,5},{13,9},{6,2},{10,6},{14,10},{7,3},{... | collective-permute-start | bytes 147464 | tf_op jit(solution)/shard_map/ppermute | solution.py:21
  15.6 0.7 %copy-start.3 = (f32[4,8,128]{2,1,0:T(8,128)S(1)}, f32[4,8,128]{2,1,0:T(8,128)}, u32[]{:S(2)}) copy-start(f32[4,8,128]{2,1,0:T(8,128)} %param.7) | copy-start | bytes 49156
  16.3 13.4 %collective-permute-start.5 = (f32[8,3,8,128]{3,2,1,0:T(8,128)S(1)}, f32[8,3,8,128]{3,2,1,0:T(8,128)S(1)}, u32[]{:S(2)}, u32[]{:S(2)}) collective-permute-start(f32[8,3,8,128]{3,2,1,0:T(8,128)S(1)} %get-tuple-element.356), channel_id=1, source_target_pairs={{0,1},{1,2},{2,3},{3,0},{4,5},{5,6},{6,7},{7,4},{8,9},{9,10},{10,1... | collective-permute-start | bytes 294920 | tf_op jit(solution)/shard_map/ppermute | solution.py:18
  17.7 12.0 %collective-permute-start.6 = (f32[8,3,8,128]{3,2,1,0:T(8,128)S(1)}, f32[8,3,8,128]{3,2,1,0:T(8,128)S(1)}, u32[]{:S(2)}, u32[]{:S(2)}) collective-permute-start(f32[8,3,8,128]{3,2,1,0:T(8,128)S(1)} %get-tuple-element.355), channel_id=1, source_target_pairs={{1,0},{2,1},{3,2},{0,3},{5,4},{6,5},{7,6},{4,7},{9,8},{10,9},{11,1... | collective-permute-start | bytes 294920 | tf_op jit(solution)/shard_map/ppermute | solution.py:21
  25.5 0.7 %copy-start.4 = (f32[5]{0:T(128)S(1)}, f32[5]{0:T(128)}, u32[]{:S(2)}) copy-start(f32[5]{0:T(128)} %constant.200.clone) | copy-start | bytes 64
where the time goes:
time: 33 us; the launch traced here: 32.6 us
  starting transfers between devices  15.9 us (48%)
  other arithmetic  11.4 us (35%)
  local copies, waits for them, and re-layouts  3.57 us (11%)
  between operations  1.69 us (5%)
    ppermute x3, starting transfers between devices, padded(): lax.ppermute(lax.slice_in_dim(block, block.shape[dim] - width, None, axis...  10.5 us
    unnamed x100, other arithmetic  5.45 us
    ppermute x3, starting transfers between devices, padded(): lax.ppermute(lax.slice_in_dim(block, 0, width, axis=dim), axis, backward)  5.3 us
    add x3, other arithmetic, interface_flux(): combined = weno_side(upwind[0:5]) + weno_side(downwind[5:0:-1])  2.2 us
    unnamed x12, local copies, waits for them, and re-layouts  1.23 us
    another operation x21, other arithmetic, project_left(): jnp.stack([sum((matrix[member][second] * vector[second] for second in ran...  1.12 us
    slice x1, local copies, waits for them, and re-layouts, local(): metrics[0:3]  0.89 us
    add x1, other arithmetic, local(): return (conserved + STEP_SIZE * time_rate, time_rate)  0.76 us
  transfers between devices with their start and end apart: 7, of which 0 were waited for; matrix products, arithmetic and copies ran while one was open for 29% of the time, Pallas kernels for 0%

commit v1 on v0

v1 whole, which is shorter than its diff:
```python
import functools

import jax
import jax.numpy as jnp
from jax import lax
from jax.experimental import pallas as pl
from jax.experimental.pallas import tpu as pltpu
from jax.sharding import PartitionSpec as P

GAMMA = 1.4
WENO_EPS = 1e-06
STEP_SIZE = 0.08
MESH = pl.DeviceIdType.MESH
F32 = jnp.float32

Z_DOWN, Z_UP, Y_DOWN, Y_UP, MIRROR, X_DOWN, X_UP, N_SEMS = 0, 3, 6, 9, 12, 15, 16, 17


def recip(value):
    return 1.0 / value


def dot3(first, second):
    return first[0] * second[0] + first[1] * second[1] + first[2] * second[2]


def cell_terms(flow, row):
    density, momentum, energy = flow[0], flow[1:4], flow[4]
    inverse = recip(density)
    velocity = [part * inverse for part in momentum]
    pressure = (GAMMA - 1.0) * energy - (0.5 * (GAMMA - 1.0)) * dot3(momentum, velocity)
    contra = dot3(row, velocity)
    flux = [density * contra]
    flux += [momentum[j] * contra + row[j] * pressure for j in range(3)]
    flux += [(energy + pressure) * contra]
    squared = (GAMMA * pressure * inverse) * dot3(row, row)
    speed = jnp.abs(contra) + squared * lax.rsqrt(squared)
    return velocity, pressure, flux, speed


def weno_part(d0, d1, d2, d3):
    x0, x1, x2 = d1 - d0, d2 - d1, d3 - d2
    e1, e2 = 0.75 * d1, 0.75 * d2
    eps = 3.0 * WENO_EPS
    b0 = (x0 * x0 + eps) + e1 * (x0 + d1)
    b1 = (x1 * x1 + eps) + e1 * d2
    b2 = (x2 * x2 + eps) + e2 * (d2 - x2)
    t12, t02, t01 = b1 * b2, b0 * b2, b0 * b1
    s12, s02, s01 = t12 * t12, t02 * t02, t01 * t01
    w2 = 1.5 * s01
    total = (s12 + 6.0 * s02) + (w2 + w2)
    top = s12 * (x0 - x1) + w2 * (x1 - x2)
    return top * recip(total)


def face_flux(d_flow, d_flux, flux_low, alpha, state, row, sweep):
    e, a, b = (sweep + 1) % 3, (sweep + 2) % 3, sweep
    density, velocity, pressure = state
    inverse_density = recip(density)
    sound2 = GAMMA * pressure * inverse_density
    inverse_sound = lax.rsqrt(sound2)
    sound = sound2 * inverse_sound
    inverse_size = lax.rsqrt(dot3(row, row))
    normal = [row[j] * inverse_size for j in range(3)]
    cross_size = lax.rsqrt(row[a] * row[a] + row[b] * row[b])
    l_a, l_b = row[b] * cross_size, -(row[a] * cross_size)
    m_e = normal[a] * l_b - normal[b] * l_a
    m_a = -(normal[e] * l_b)
    m_b = normal[e] * l_a
    kinetic = 0.5 * dot3(velocity, velocity)
    half_factor = (0.5 * (GAMMA - 1.0)) * inverse_sound * inverse_sound
    half_normal = [(0.5 * inverse_sound) * normal[j] for j in range(3)]

    def project(vector):
        rho = vector[0]
        w = [vector[1 + j] - velocity[j] * rho for j in range(3)]
        half_a = half_factor * ((vector[4] - kinetic * rho) - dot3(velocity, w))
        half_n = dot3(half_normal, w)
        return [
            half_a - half_n,
            rho - (half_a + half_a),
            l_a * w[a] + l_b * w[b],
            m_e * w[e] + m_a * w[a] + m_b * w[b],
            half_a + half_n,
        ]

    scaled = [[alpha * d_flow(m, c) for c in range(5)] for m in range(5)]
    ups = [[scaled[m][c] + d_flux(m, c) for c in range(5)] for m in range(4)]
    downs = [[scaled[m][c] - d_flux(m, c) for c in range(5)] for m in range(1, 5)]
    up_chars = [project(vector) for vector in ups]
    down_chars = [project(vector) for vector in downs]
    chars = [
        weno_part(*[up_chars[m][r] for m in range(4)])
        + weno_part(*[down_chars[m][r] for m in (3, 2, 1, 0)])
        for r in range(5)
    ]
    both = chars[0] + chars[4]
    carried = sound * (chars[4] - chars[0])
    mass = both + chars[1]
    enthalpy = sound2 * (1.0 / (GAMMA - 1.0)) + kinetic
    tangent_speed = l_a * velocity[a] + l_b * velocity[b]
    binormal_speed = m_e * velocity[e] + m_a * velocity[a] + m_b * velocity[b]
    right = [None] * 5
    right[0] = mass
    right[1 + e] = velocity[e] * mass + normal[e] * carried + m_e * chars[3]
    right[1 + a] = (velocity[a] * mass + normal[a] * carried) + (l_a * chars[2] + m_a * chars[3])
    right[1 + b] = (velocity[b] * mass + normal[b] * carried) + (l_b * chars[2] + m_b * chars[3])
    right[4] = (enthalpy * both + kinetic * chars[1]) + (
        (tangent_speed * chars[2] + binormal_speed * chars[3]) + dot3(normal, velocity) * carried
    )
    return [
        (flux_low[c] + 0.5 * d_flux(2, c))
        + (1.0 / 6.0) * ((0.5 * (ups[1][c] + downs[2][c]) - scaled[2][c]) + right[c])
        for c in range(5)
    ]


def line_sweep(cells, terms, faces, sweep, width):
    def prepare(k, _):
        flow = [cells[c, k] for c in range(5)]
        row = [cells[5 + j, k] for j in range(3)]
        velocity, pressure, flux, speed = cell_terms(flow, row)
        for c in range(5):
            terms[c, k] = flux[c]
        terms[5, k] = speed
        for j in range(3):
            terms[6 + j, k] = velocity[j]
        terms[9, k] = pressure
        return _

    lax.fori_loop(0, width + 6, prepare, 0)

    def one_face(k, _):
        alpha = terms[5, k]
        for m in range(1, 6):
            alpha = jnp.maximum(alpha, terms[5, k + m])
        density = 0.5 * (cells[0, k + 2] + cells[0, k + 3])
        velocity = [0.5 * (terms[6 + j, k + 2] + terms[6 + j, k + 3]) for j in range(3)]
        pressure = 0.5 * (terms[9, k + 2] + terms[9, k + 3])
        row = [0.5 * (cells[5 + j, k + 2] + cells[5 + j, k + 3]) for j in range(3)]
        flux = face_flux(
            lambda m, c: cells[c, k + m + 1] - cells[c, k + m],
            lambda m, c: terms[c, k + m + 1] - terms[c, k + m],
            [terms[c, k + 2] for c in range(5)],
            alpha,
            (density, velocity, pressure),
            row,
            sweep,
        )
        for c in range(5):
            faces[c, k] = flux[c]
        return _

    lax.fori_loop(0, width + 1, one_face, 0)


def lane_sweep(flow, row, sweep):
    lanes = flow[0].shape[-1]

    def ahead(value, shift):
        return pltpu.roll(value, (-shift) % lanes, 1)

    velocity, pressure, flux, speed = cell_terms(flow, row)
    pair = jnp.maximum(speed, ahead(speed, 1))
    alpha = jnp.maximum(jnp.maximum(pair, ahead(pair, -2)), ahead(pair, 2))
    mean = lambda value: 0.5 * (value + ahead(value, 1))
    state = (mean(flow[0]), [mean(part) for part in velocity], mean(pressure))
    row_mean = [mean(part) for part in row]
    d_flow = [ahead(part, 1) - part for part in flow]
    d_flux = [ahead(part, 1) - part for part in flux]
    shifted_flow = [[part if m == 2 else ahead(part, m - 2) for part in d_flow] for m in range(5)]
    shifted_flux = [[part if m == 2 else ahead(part, m - 2) for part in d_flux] for m in range(5)]
    return face_flux(
        lambda m, c: shifted_flow[m][c],
        lambda m, c: shifted_flux[m][c],
        flux,
        alpha,
        state,
        row_mean,
        sweep,
    )


def swap_blocks(values, sublane):
    def exchange(first, second, step):
        high = (sublane // step) % 2 == 1
        return (
            jnp.where(high, pltpu.roll(second, step, 0), first),
            jnp.where(high, second, pltpu.roll(first, 8 - step, 0)),
        )

    v0, v1, v2, v3 = values
    v0, v2 = exchange(v0, v2, 2)
    v1, v3 = exchange(v1, v3, 2)
    v0, v1 = exchange(v0, v1, 1)
    v2, v3 = exchange(v2, v3, 1)
    return [v0, v1, v2, v3]


def kernel(
    shape,
    flow_ref,
    metrics_ref,
    wake_ref,
    out_ref,
    zv,
    ym,
    xm,
    wake,
    yv,
    mirror,
    edge,
    edge_low,
    edge_high,
    terms,
    faces,
    x_faces,
    load_sem,
    send_sem,
    recv_sem,
):
    nx, ny, nz = shape
    planes, rows, lanes = flow_ref.shape[1:]
    ix, iy, iz = lax.axis_index("gx"), lax.axis_index("gy"), lax.axis_index("gz")
    partner = nx - 1 - ix
    has_left, has_right = ix > 0, ix < nx - 1
    at_wall, at_top = iy == 0, iy == ny - 1
    z_low = {"gz": lax.rem(iz + nz - 1, nz)}
    z_high = {"gz": lax.rem(iz + 1, nz)}

    barrier = pltpu.get_barrier_semaphore()

    def greet(target):
        pl.semaphore_signal(barrier, inc=1, device_id=target, device_id_type=MESH)

    greet(z_low)
    greet(z_high)
    expected = 2

    @pl.when(has_left)
    def _():
        greet({"gx": ix - 1})

    @pl.when(has_right)
    def _():
        greet({"gx": ix + 1})

    @pl.when(at_wall)
    def _():
        greet({"gx": partner})

    @pl.when(jnp.logical_not(at_wall))
    def _():
        greet({"gy": iy - 1})

    @pl.when(jnp.logical_not(at_top))
    def _():
        greet({"gy": iy + 1})

    own_z = zv.at[:, 3 : 3 + planes]
    loads = [
        pltpu.make_async_copy(flow_ref, zv.at[0:5, 3 : 3 + planes], load_sem.at[0]),
        pltpu.make_async_copy(metrics_ref.at[6:9], zv.at[5:8, 3 : 3 + planes], load_sem.at[1]),
        pltpu.make_async_copy(metrics_ref.at[0:3], xm, load_sem.at[2]),
        pltpu.make_async_copy(metrics_ref.at[3:6], ym, load_sem.at[3]),
        pltpu.make_async_copy(wake_ref, wake, load_sem.at[4]),
    ]
    for copy in loads:
        copy.start()
    for copy in loads:
        copy.wait()

    lane = lax.broadcasted_iota(jnp.int32, (rows, lanes), 1)
    sublane = lax.broadcasted_iota(jnp.int32, (rows, lanes), 0)

    def source(c, p):
        return zv[c, 3 + p] if c < 5 else xm[c - 5, p]

    for c in range(8):
        packed = source(c, planes - 1)
        for p in range(planes):
            value = source(c, p)
            low = pltpu.roll(value, 16 * p + 3, 1)
            high = pltpu.roll(value, (16 * p + 13) % lanes, 1)
            packed = jnp.where((lane >= 16 * p + 3) & (lane < 16 * p + 8), low, packed)
            packed = jnp.where((lane >= 16 * p + 8) & (lane < 16 * p + 13), high, packed)
        edge[c] = packed

    expected = (
        3
        + has_left.astype(jnp.int32)
        + has_right.astype(jnp.int32)
        + jnp.logical_not(at_top).astype(jnp.int32)
    )
    pl.semaphore_wait(barrier, expected)

    def remote(src, dst, index, target):
        return pltpu.make_async_remote_copy(
            src_ref=src,
            dst_ref=dst,
            send_sem=send_sem.at[index],
            recv_sem=recv_sem.at[index],
            device_id=target,
            device_id_type=MESH,
        )

    z_copies = []
    for j in range(3):
        z_copies.append(remote(zv.at[:, 3 + j], zv.at[:, 3 + planes + j], Z_DOWN + j, z_low))
        z_copies.append(
            remote(zv.at[:, 2 + planes - j], zv.at[:, 2 - j], Z_UP + j, z_high)
        )
    for copy in z_copies:
        copy.start()

    x_down = remote(edge, edge_high, X_DOWN, {"gx": ix - 1})
    x_up = remote(edge, edge_low, X_UP, {"gx": ix + 1})

    @pl.when(has_left)
    def _():
        x_down.start()

    @pl.when(has_right)
    def _():
        x_up.start()

    def y_copies(kind):
        copies = []
        for j in range(3):
            if kind == "down":
                index, target, cell = Y_DOWN + j, {"gy": iy - 1}, j
                flow_dst = lambda lo, hi: yv.at[lo:hi, 7 + j, 4:8, :]
            elif kind == "up":
                index, target, cell = Y_UP + j, {"gy": iy + 1}, rows - 3 + j
                flow_dst = lambda lo, hi: yv.at[lo:hi, j, 0:4, :]
            else:
                index, target, cell = MIRROR + j, {"gx": partner}, j
                flow_dst = lambda lo, hi: mirror.at[lo:hi, j, 0:4, :]
            copies.append(
                pltpu.make_async_remote_copy(
                    src_ref=zv.at[0:5, 3 : 3 + planes, cell, :],
                    dst_ref=flow_dst(0, 5),
                    send_sem=send_sem.at[index],
                    recv_sem=recv_sem.at[index],
                    device_id=target,
                    device_id_type=MESH,
                )
            )
            copies.append(
                pltpu.make_async_remote_copy(
                    src_ref=ym.at[:, :, cell, :],
                    dst_ref=flow_dst(5, 8),
                    send_sem=send_sem.at[N_SEMS + index],
                    recv_sem=recv_sem.at[N_SEMS + index],
                    device_id=target,
                    device_id_type=MESH,
                )
            )
        return copies

    y_down, y_up, to_mirror = y_copies("down"), y_copies("up"), y_copies("mirror")

    @pl.when(at_wall)
    def _():
        for copy in to_mirror:
            copy.start()

    @pl.when(jnp.logical_not(at_wall))
    def _():
        for copy in y_down:
            copy.start()

    @pl.when(jnp.logical_not(at_top))
    def _():
        for copy in y_up:
            copy.start()

    def x_plane(p, _):
        flux = lane_sweep([zv[c, 3 + p] for c in range(5)], [xm[j, p] for j in range(3)], 0)
        for c in range(5):
            x_faces[c, p] = flux[c]
        return _

    lax.fori_loop(0, planes, x_plane, 0)

    lower_half = sublane < 4
    for c in range(8):
        swapped = swap_blocks(
            [zv[c, 3 + p] if c < 5 else ym[c - 5, p] for p in range(planes)], sublane
        )
        for k in range(4):
            yv[c, 3 + k] = swapped[k]
        for k in range(3):
            yv[c, k, 4:8] = swapped[1 + k][0:4]
            yv[c, 7 + k, 0:4] = swapped[k][4:8]

    @pl.when(jnp.logical_not(at_top))
    def _():
        for copy in y_down:
            copy.wait_recv()

    @pl.when(at_top)
    def _():
        for c in range(8):
            for k in range(3):
                yv[c, 7 + k, 4:8] = yv[c, 6, 4:8]

    @pl.when(jnp.logical_not(at_wall))
    def _():
        for copy in y_up:
            copy.wait_recv()

    @pl.when(at_wall)
    def _():
        for copy in to_mirror:
            copy.wait_recv()
        is_wake = jnp.broadcast_to(wake[...], (rows, lanes)) >= 0
        backwards = (lanes - 1) - lane
        for c in range(8):
            for k in range(3):
                facing = jnp.take_along_axis(
                    mirror[c, k], backwards, axis=1, mode="promise_in_bounds"
                )
                here = yv[c, 3 + k]
                if 1 <= c <= 3:
                    here = -here
                yv[c, 2 - k, 0:4] = jnp.where(is_wake, facing, here)[0:4]

    line_sweep(yv, terms, faces, 1, 4)
    y_parts = []
    for c in range(5):
        y_parts.append(
            swap_blocks([faces[c, k + 1] - faces[c, k] for k in range(4)], sublane)
        )
    for c in range(5):
        for p in range(planes):
            out_ref[c, p] = y_parts[c][p]

    @pl.when(has_left)
    def _():
        x_up.wait_recv()

    @pl.when(jnp.logical_not(has_left))
    def _():
        for c in range(8):
            for k in range(3):
                moved = pltpu.roll(edge[c], 7 + k, 1)
                edge_low[c] = moved if k == 0 else jnp.where(lane % 16 == 10 + k, moved, edge_low[c])

    @pl.when(has_right)
    def _():
        x_down.wait_recv()

    @pl.when(jnp.logical_not(has_right))
    def _():
        for c in range(8):
            for k in range(3):
                moved = pltpu.roll(edge[c], (3 + k - 12) % lanes, 1)
                edge_high[c] = moved if k == 0 else jnp.where(lane % 16 == 3 + k, moved, edge_high[c])

    place = lane % 16
    ends = []
    for c in range(8):
        value = jnp.where(place < 3, pltpu.roll(edge_low[c], lanes - 10, 1), edge[c])
        value = jnp.where(place >= 13, pltpu.roll(edge_high[c], 10, 1), value)
        ends.append(value)
    ends = lane_sweep(ends[0:5], ends[5:8], 0)
    for c in range(5):
        for p in range(planes):
            low = pltpu.roll(ends[c], (-(16 * p + 3)) % lanes, 1)
            high = pltpu.roll(ends[c], (lanes - 3 - (16 * p + 10)) % lanes, 1)
            upper = jnp.where(lane < 2, low, jnp.where(lane >= lanes - 3, high, x_faces[c, p]))
            lower = pltpu.roll(jnp.where(lane == lanes - 1, low, upper), 1, 1)
            out_ref[c, p] = out_ref[c, p] + (upper - lower)

    for copy in z_copies:
        copy.wait_recv()
    line_sweep(zv, terms, faces, 2, planes)
    for c in range(5):
        for p in range(planes):
            out_ref[c, p] = out_ref[c, p] + (faces[c, p + 1] - faces[c, p])

    for copy in z_copies:
        copy.wait_send()

    @pl.when(has_left)
    def _():
        x_down.wait_send()

    @pl.when(has_right)
    def _():
        x_up.wait_send()

    @pl.when(at_wall)
    def _():
        for copy in to_mirror:
            copy.wait_send()

    @pl.when(jnp.logical_not(at_wall))
    def _():
        for copy in y_down:
            copy.wait_send()

    @pl.when(jnp.logical_not(at_top))
    def _():
        for copy in y_up:
            copy.wait_send()


def solution(mesh):
    nx, ny, nz = mesh.shape["gx"], mesh.shape["gy"], mesh.shape["gz"]

    def local(conserved, metrics, inv_volume, wake_donor):
        planes, rows, lanes = conserved.shape[1:]
        tile = (rows, lanes)
        summed = pl.pallas_call(
            functools.partial(kernel, (nx, ny, nz)),
            out_shape=jax.ShapeDtypeStruct(conserved.shape, F32),
            in_specs=[pl.BlockSpec(memory_space=pl.ANY)] * 3,
            out_specs=pl.BlockSpec(memory_space=pltpu.VMEM),
            scratch_shapes=[
                pltpu.VMEM((8, planes + 6) + tile, F32),
                pltpu.VMEM((3, planes) + tile, F32),
                pltpu.VMEM((3, planes) + tile, F32),
                pltpu.VMEM((1, lanes), jnp.int32),
                pltpu.VMEM((8, 10) + tile, F32),
                pltpu.VMEM((8, 3) + tile, F32),
                pltpu.VMEM((8,) + tile, F32),
                pltpu.VMEM((8,) + tile, F32),
                pltpu.VMEM((8,) + tile, F32),
                pltpu.VMEM((10, 10) + tile, F32),
                pltpu.VMEM((5, 5) + tile, F32),
                pltpu.VMEM((5, planes) + tile, F32),
                pltpu.SemaphoreType.DMA((5,)),
                pltpu.SemaphoreType.DMA((2 * N_SEMS,)),
                pltpu.SemaphoreType.DMA((2 * N_SEMS,)),
            ],
            compiler_params=pltpu.CompilerParams(collective_id=0, has_side_effects=True),
            cost_estimate=pl.CostEstimate(
                flops=60_000_000, bytes_accessed=500_000, transcendentals=0
            ),
        )(conserved, metrics, wake_donor.reshape(1, lanes))
        time_rate = -inv_volume[None] * summed
        return (conserved + STEP_SIZE * time_rate, time_rate)

    placed = (P(None, "gz", "gy", "gx"), P(None, "gz", "gy", "gx"), P("gz", "gy", "gx"), P("gx"))
    return jax.shard_map(
        local,
        mesh=mesh,
        in_specs=placed,
        out_specs=(P(None, "gz", "gy", "gx"), P(None, "gz", "gy", "gx")),
        check_vma=False,
    )
```

time: 33 us -> 17.2 us (0.52)
  the two profiles are of different devices: /device:TPU:1 before, /device:TPU:0 now
where the time goes in v1:
time: 17.2 us; the launch traced here: 17 us
  Pallas kernels  14 us (81%)
  other arithmetic  2.28 us (13%)
  between operations  0.65 us (4%)
    pallas_call x1, Pallas kernels, local(): pl.pallas_call(functools.partial(kernel, (nx, ny, nz)), out_shape=jax.Sha...  14 us
    add x1, other arithmetic, local(): return (conserved + STEP_SIZE * time_rate, time_rate)  1.56 us
    neg x1, other arithmetic, local(): time_rate = -inv_volume[None] * summed  0.72 us

profile of v1, /device:TPU:0, one launch (start us, length us, event | category | flops | bytes accessed | tf_op | source)
XLA Modules:
  0.0 17.0 jit_solution(14169001559906150996)
XLA Ops:
  0.6 0.7 %neg.4 = f32[4,8,128]{2,1,0:T(8,128)S(1)} negate(f32[4,8,128]{2,1,0:T(8,128)} %param.6) | non-fusion elementwise | flops 4096 | bytes 32768 | tf_op jit(solution)/shard_map/neg | solution.py:543
  1.4 0.0 copy-start
  1.4 14.0 %shard_map.59 = f32[5,4,8,128]{3,2,1,0:T(8,128)} custom-call(f32[5,4,8,128]{3,2,1,0:T(8,128)} %flow_ref.1, f32[9,4,8,128]{3,2,1,0:T(8,128)} %metrics_ref.1, s32[1,128]{1,0:T(1,128)} %bitcast.1), custom_call_target="tpu_custom_call" | custom-call | flops 60000000 | bytes 500000 | tf_op jit(solution)/shard_map/pallas_call | solution.py:516
  15.4 0.0 copy-done
  15.4 1.6 %multiply_add_fusion = (f32[5,4,8,128]{3,2,1,0:T(8,128)}, f32[5,4,8,128]{3,2,1,0:T(8,128)}) fusion(f32[5,4,8,128]{3,2,1,0:T(8,128)S(1)} %copy-done, f32[5,4,8,128]{3,2,1,0:T(8,128)} %shard_map.59, f32[4,8,128]{2,1,0:T(8,128)S(1)} %neg.4), kind=kLoop, calls=%fused_computation | loop fusion | flops 61440 | bytes 344064 | tf_op jit(solution)/shard_map/add | solution.py:544
Async XLA Ops:
  1.4 14.0 %copy-start = (f32[5,4,8,128]{3,2,1,0:T(8,128)S(1)}, f32[5,4,8,128]{3,2,1,0:T(8,128)}, u32[]{:S(2)}) copy-start(f32[5,4,8,128]{3,2,1,0:T(8,128)} %flow_ref.1) | copy-start | bytes 245764

commit v2 on v1

--- a/solution.py
+++ b/solution.py
@@ -13,7 +13,7 @@
 MESH = pl.DeviceIdType.MESH
 F32 = jnp.float32
 
-Z_DOWN, Z_UP, Y_DOWN, Y_UP, MIRROR, X_DOWN, X_UP, N_SEMS = 0, 3, 6, 9, 12, 15, 16, 17
+Z_DOWN, Z_UP, Y_DOWN, Y_UP, MIRROR, X_DOWN, X_UP, Z_LAST, RELAY, N_SEMS = 0, 3, 6, 9, 12, 15, 16, 17, 18, 21
 
 
 def recip(value):
@@ -115,7 +115,7 @@
     ]
 
 
-def line_sweep(cells, terms, faces, sweep, width):
+def line_steps(cells, terms, faces, sweep):
     def prepare(k, _):
         flow = [cells[c, k] for c in range(5)]
         row = [cells[5 + j, k] for j in range(3)]
@@ -127,8 +127,6 @@
             terms[6 + j, k] = velocity[j]
         terms[9, k] = pressure
         return _
-
-    lax.fori_loop(0, width + 6, prepare, 0)
 
     def one_face(k, _):
         alpha = terms[5, k]
@@ -151,7 +149,7 @@
             faces[c, k] = flux[c]
         return _
 
-    lax.fori_loop(0, width + 1, one_face, 0)
+    return prepare, one_face
 
 
 def lane_sweep(flow, row, sweep):
@@ -204,6 +202,7 @@
     wake_ref,
     out_ref,
     zv,
+    relay,
     ym,
     xm,
     wake,
@@ -215,6 +214,7 @@
     terms,
     faces,
     x_faces,
+    ready,
     load_sem,
     send_sem,
     recv_sem,
@@ -233,31 +233,26 @@
     def greet(target):
         pl.semaphore_signal(barrier, inc=1, device_id=target, device_id_type=MESH)
 
-    greet(z_low)
-    greet(z_high)
-    expected = 2
-
-    @pl.when(has_left)
-    def _():
-        greet({"gx": ix - 1})
-
-    @pl.when(has_right)
-    def _():
-        greet({"gx": ix + 1})
-
-    @pl.when(at_wall)
-    def _():
-        greet({"gx": partner})
-
-    @pl.when(jnp.logical_not(at_wall))
-    def _():
-        greet({"gy": iy - 1})
-
-    @pl.when(jnp.logical_not(at_top))
-    def _():
-        greet({"gy": iy + 1})
-
-    own_z = zv.at[:, 3 : 3 + planes]
+    is_first, is_second, is_last = iz == 0, iz == 1, iz == nz - 1
+    mirror_up = at_wall & (partner > ix)
+    mirror_down = at_wall & (partner < ix)
+    not_first, not_last = jnp.logical_not(is_first), jnp.logical_not(is_last)
+    not_wall, not_top = jnp.logical_not(at_wall), jnp.logical_not(at_top)
+    x_low, x_high = {"gx": ix - 1}, {"gx": ix + 1}
+    y_low, y_high = {"gy": iy - 1}, {"gy": iy + 1}
+    opposite = {"gx": partner}
+
+    def when(condition, action):
+        pl.when(condition)(action)
+
+    when(not_last, lambda: greet(z_high))
+    when(is_first | is_second, lambda: greet({"gz": nz - 1}))
+    when(has_right, lambda: greet(x_high))
+    when(not_top, lambda: greet(y_high))
+    when(mirror_up, lambda: greet(opposite))
+    other_core = lax.rem(iy, 2) == 1
+    when(other_core, lambda: greet(y_low))
+
     loads = [
         pltpu.make_async_copy(flow_ref, zv.at[0:5, 3 : 3 + planes], load_sem.at[0]),
         pltpu.make_async_copy(metrics_ref.at[6:9], zv.at[5:8, 3 : 3 + planes], load_sem.at[1]),
@@ -267,11 +262,76 @@
     ]
     for copy in loads:
         copy.start()
-    for copy in loads:
-        copy.wait()
+    as_int = lambda flag: flag.astype(jnp.int32)
+    pl.semaphore_wait(
+        barrier,
+        as_int(not_first)
+        + 2 * as_int(is_last)
+        + as_int(has_left)
+        + as_int(not_wall)
+        + as_int(mirror_down)
+        + as_int(not_top & jnp.logical_not(other_core)),
+    )
+
+    def tell(index, target):
+        pl.semaphore_signal(ready.at[index], inc=1, device_id=target, device_id_type=MESH)
+
+    def hear(index):
+        pl.semaphore_wait(ready.at[index], 1)
+
+    when(not_first, lambda: tell(0, z_low))
+    when(is_last, lambda: tell(1, {"gz": 1}))
+    when(has_left, lambda: tell(2, x_low))
+    when(not_wall, lambda: tell(3, y_low))
+    when(mirror_down, lambda: tell(4, opposite))
 
     lane = lax.broadcasted_iota(jnp.int32, (rows, lanes), 1)
     sublane = lax.broadcasted_iota(jnp.int32, (rows, lanes), 0)
+
+    def remote(src, dst, index, target):
+        return pltpu.make_async_remote_copy(
+            src_ref=src,
+            dst_ref=dst,
+            send_sem=send_sem.at[index],
+            recv_sem=recv_sem.at[index],
+            device_id=target,
+            device_id_type=MESH,
+        )
+
+    def up_copy(j):
+        return remote(zv.at[:, 2 + planes - j], zv.at[:, 2 - j], Z_UP + j, z_high)
+
+    def down_copy(j):
+        return remote(zv.at[:, 3 + j], zv.at[:, 3 + planes + j], Z_DOWN + j, z_low)
+
+    def relay_copy(j):
+        return pltpu.make_async_remote_copy(
+            src_ref=relay if j == 0 else zv.at[:, j - 1],
+            dst_ref=zv.at[:, 3 + planes + j],
+            send_sem=send_sem.at[RELAY + j],
+            recv_sem=recv_sem.at[Z_DOWN + j],
+            device_id={"gz": nz - 1},
+            device_id_type=MESH,
+        )
+
+    extra = remote(zv.at[:, 3], relay, Z_LAST, z_high)
+    ups = [up_copy(j) for j in range(3)]
+    downs = [down_copy(j) for j in range(3)]
+    relays = [relay_copy(j) for j in range(3)]
+
+    def start(copies):
+        def action():
+            for copy in copies:
+                copy.start()
+
+        return action
+
+    for copy in loads[0:2]:
+        copy.wait()
+    when(is_last & jnp.logical_not(other_core), start(ups))
+    when(not_first & not_last, start(downs))
+    for copy in loads[2:]:
+        copy.wait()
 
     def source(c, p):
         return zv[c, 3 + p] if c < 5 else xm[c - 5, p]
@@ -286,43 +346,9 @@
             packed = jnp.where((lane >= 16 * p + 8) & (lane < 16 * p + 13), high, packed)
         edge[c] = packed
 
-    expected = (
-        3
-        + has_left.astype(jnp.int32)
-        + has_right.astype(jnp.int32)
-        + jnp.logical_not(at_top).astype(jnp.int32)
-    )
-    pl.semaphore_wait(barrier, expected)
-
-    def remote(src, dst, index, target):
-        return pltpu.make_async_remote_copy(
-            src_ref=src,
-            dst_ref=dst,
-            send_sem=send_sem.at[index],
-            recv_sem=recv_sem.at[index],
-            device_id=target,
-            device_id_type=MESH,
-        )
-
-    z_copies = []
-    for j in range(3):
-        z_copies.append(remote(zv.at[:, 3 + j], zv.at[:, 3 + planes + j], Z_DOWN + j, z_low))
-        z_copies.append(
-            remote(zv.at[:, 2 + planes - j], zv.at[:, 2 - j], Z_UP + j, z_high)
-        )
-    for copy in z_copies:
-        copy.start()
-
-    x_down = remote(edge, edge_high, X_DOWN, {"gx": ix - 1})
-    x_up = remote(edge, edge_low, X_UP, {"gx": ix + 1})
-
-    @pl.when(has_left)
-    def _():
-        x_down.start()
-
-    @pl.when(has_right)
-    def _():
-        x_up.start()
+    x_down = remote(edge, edge_high, X_DOWN, x_low)
+    x_up = remote(edge, edge_low, X_UP, x_high)
+    when(has_left, x_down.start)
 
     def y_copies(kind):
         copies = []
@@ -360,20 +386,8 @@
 
     y_down, y_up, to_mirror = y_copies("down"), y_copies("up"), y_copies("mirror")
 
-    @pl.when(at_wall)
-    def _():
-        for copy in to_mirror:
-            copy.start()
-
-    @pl.when(jnp.logical_not(at_wall))
-    def _():
-        for copy in y_down:
-            copy.start()
-
-    @pl.when(jnp.logical_not(at_top))
-    def _():
-        for copy in y_up:
-            copy.start()
+    when(not_wall, start(y_down))
+    when(mirror_down, start(to_mirror))
 
     def x_plane(p, _):
         flux = lane_sweep([zv[c, 3 + p] for c in range(5)], [xm[j, p] for j in range(3)], 0)
@@ -382,6 +396,39 @@
         return _
 
     lax.fori_loop(0, planes, x_plane, 0)
+
+    when(is_last & other_core, start(ups))
+
+    @pl.when(not_last)
+    def _():
+        hear(0)
+        when(is_first, extra.start)
+        start([ups[2], ups[1], ups[0]])()
+
+    @pl.when(mirror_up)
+    def _():
+        hear(4)
+        start(to_mirror)()
+
+    @pl.when(not_top)
+    def _():
+        hear(3)
+        start(y_up)()
+
+    @pl.when(has_right)
+    def _():
+        hear(2)
+        x_up.start()
+
+    @pl.when(is_second)
+    def _():
+        extra.wait_recv()
+        for copy in ups:
+            copy.wait_recv()
+        hear(1)
+        start(relays)()
+
+    when(is_last, start(downs))
 
     lower_half = sublane < 4
     for c in range(8):
@@ -426,11 +473,13 @@
                     here = -here
                 yv[c, 2 - k, 0:4] = jnp.where(is_wake, facing, here)[0:4]
 
-    line_sweep(yv, terms, faces, 1, 4)
+    prepare, one_face = line_steps(yv, terms, faces, 1)
+    lax.fori_loop(0, 10, prepare, 0)
+    lax.fori_loop(0, 5, one_face, 0)
     y_parts = []
     for c in range(5):
         y_parts.append(
-            swap_blocks([faces[c, k + 1] - faces[c, k] for k in range(4)], sublane)
+            swap_blocks([faces[c, k] - faces[c, k + 1] for k in range(4)], sublane)
         )
     for c in range(5):
         for p in range(planes):
@@ -471,17 +520,52 @@
             high = pltpu.roll(ends[c], (lanes - 3 - (16 * p + 10)) % lanes, 1)
             upper = jnp.where(lane < 2, low, jnp.where(lane >= lanes - 3, high, x_faces[c, p]))
             lower = pltpu.roll(jnp.where(lane == lanes - 1, low, upper), 1, 1)
-            out_ref[c, p] = out_ref[c, p] + (upper - lower)
-
-    for copy in z_copies:
+            out_ref[c, p] = out_ref[c, p] + (lower - upper)
+
+    prepare, one_face = line_steps(zv, terms, faces, 2)
+    lax.fori_loop(3, 3 + planes, prepare, 0)
+    for copy in downs:
         copy.wait_recv()
-    line_sweep(zv, terms, faces, 2, planes)
-    for c in range(5):
-        for p in range(planes):
-            out_ref[c, p] = out_ref[c, p] + (faces[c, p + 1] - faces[c, p])
-
-    for copy in z_copies:
+    lax.fori_loop(3 + planes, 6 + planes, prepare, 0)
+
+    def finish(k, _):
+        for c in range(5):
+            out_ref[c, k] = out_ref[c, k] + (faces[c, k] - faces[c, k + 1])
+        return _
+
+    lax.fori_loop(3, planes + 1, one_face, 0)
+    lax.fori_loop(3, planes, finish, 0)
+
+    def near_face(j, carry):
+        k = 2 - j
+
+        @pl.when(jnp.logical_not(is_second))
+        def _():
+            up_copy(j).wait_recv()
+
+        prepare(k, 0)
+        one_face(k, 0)
+        finish(k, 0)
+        return carry
+
+    lax.fori_loop(0, 3, near_face, 0)
+
+    for copy in ups:
         copy.wait_send()
+
+    @pl.when(is_first)
+    def _():
+        extra.wait_send()
+
+    @pl.when(jnp.logical_not(is_first))
+    def _():
+        for copy in downs:
+            copy.wait_send()
+
+    @pl.when(is_second)
+    def _():
+        for copy in relays:
+            copy.wait_send()
 
     @pl.when(has_left)
     def _():
@@ -513,13 +597,15 @@
     def local(conserved, metrics, inv_volume, wake_donor):
         planes, rows, lanes = conserved.shape[1:]
         tile = (rows, lanes)
+        operands = (conserved, metrics, wake_donor.reshape(1, lanes))
         summed = pl.pallas_call(
             functools.partial(kernel, (nx, ny, nz)),
             out_shape=jax.ShapeDtypeStruct(conserved.shape, F32),
-            in_specs=[pl.BlockSpec(memory_space=pl.ANY)] * 3,
+            in_specs=[pl.BlockSpec(memory_space=pltpu.HBM)] * 3,
             out_specs=pl.BlockSpec(memory_space=pltpu.VMEM),
             scratch_shapes=[
                 pltpu.VMEM((8, planes + 6) + tile, F32),
+                pltpu.VMEM((8,) + tile, F32),
                 pltpu.VMEM((3, planes) + tile, F32),
                 pltpu.VMEM((3, planes) + tile, F32),
                 pltpu.VMEM((1, lanes), jnp.int32),
@@ -531,16 +617,19 @@
                 pltpu.VMEM((10, 10) + tile, F32),
                 pltpu.VMEM((5, 5) + tile, F32),
                 pltpu.VMEM((5, planes) + tile, F32),
+                pltpu.SemaphoreType.REGULAR((5,)),
                 pltpu.SemaphoreType.DMA((5,)),
                 pltpu.SemaphoreType.DMA((2 * N_SEMS,)),
                 pltpu.SemaphoreType.DMA((2 * N_SEMS,)),
             ],
-            compiler_params=pltpu.CompilerParams(collective_id=0, has_side_effects=True),
+            compiler_params=pltpu.CompilerParams(
+                collective_id=0, has_side_effects=True, vmem_limit_bytes=8 * 1024 * 1024
+            ),
             cost_estimate=pl.CostEstimate(
                 flops=60_000_000, bytes_accessed=500_000, transcendentals=0
             ),
-        )(conserved, metrics, wake_donor.reshape(1, lanes))
-        time_rate = -inv_volume[None] * summed
+        )(*[pltpu.with_memory_space_constraint(x, pltpu.HBM) for x in operands])
+        time_rate = inv_volume[None] * summed
         return (conserved + STEP_SIZE * time_rate, time_rate)
 
     placed = (P(None, "gz", "gy", "gx"), P(None, "gz", "gy", "gx"), P("gz", "gy", "gx"), P("gx"))

time: 17.2 us -> 12.5 us (0.73)
  the two profiles are of different devices: /device:TPU:0 before, /device:TPU:28 now
where the time goes in v2:
time: 12.5 us; the launch traced here: 12.3 us
  Pallas kernels  11 us (88%)
  other arithmetic  0.68 us (5%)
  between operations  0.67 us (5%)
    pallas_call x1, Pallas kernels, local(): pl.pallas_call(functools.partial(kernel, (nx, ny, nz)), out_shape=jax.Sha...  11 us
    add x1, other arithmetic, local(): return (conserved + STEP_SIZE * time_rate, time_rate)  0.68 us

profile of v2, /device:TPU:28, one launch (start us, length us, event | category | flops | bytes accessed | tf_op | source)
XLA Modules:
  0.0 12.3 jit_solution(7677416871005577572)
XLA Ops:
  0.6 0.0 copy-start
  0.6 0.0 copy-start.1
  0.7 11.0 %shard_map.59 = f32[5,4,8,128]{3,2,1,0:T(8,128)S(1)} custom-call(f32[5,4,8,128]{3,2,1,0:T(8,128)} %flow_ref.1, f32[9,4,8,128]{3,2,1,0:T(8,128)} %metrics_ref.1, s32[1,128]{1,0:T(1,128)} %bitcast.1), custom_call_target="tpu_custom_call" | custom-call | flops 60000000 | bytes 500000 | tf_op jit(solution)/shard_map/pallas_call | solution.py:601
  11.6 0.0 copy-done
  11.6 0.0 copy-done.1
  11.7 0.7 %multiply_add_fusion = (f32[5,4,8,128]{3,2,1,0:T(8,128)}, f32[5,4,8,128]{3,2,1,0:T(8,128)}) fusion(f32[5,4,8,128]{3,2,1,0:T(8,128)S(1)} %copy-done, f32[5,4,8,128]{3,2,1,0:T(8,128)S(1)} %shard_map.59, f32[4,8,128]{2,1,0:T(8,128)S(1)} %copy-done.1), kind=kLoop, calls=%fused_computation | loop fusion | flops 61440 | bytes 344064 | tf_op jit(solution)/shard_map/add | solution.py:633
Async XLA Ops:
  0.6 11.0 %copy-start = (f32[5,4,8,128]{3,2,1,0:T(8,128)S(1)}, f32[5,4,8,128]{3,2,1,0:T(8,128)}, u32[]{:S(2)}) copy-start(f32[5,4,8,128]{3,2,1,0:T(8,128)} %flow_ref.1) | copy-start | bytes 245764
  0.6 11.0 %copy-start.1 = (f32[4,8,128]{2,1,0:T(8,128)S(1)}, f32[4,8,128]{2,1,0:T(8,128)}, u32[]{:S(2)}) copy-start(f32[4,8,128]{2,1,0:T(8,128)} %param.6) | copy-start | bytes 49156

commit v3 on v2

--- a/solution.py
+++ b/solution.py
@@ -199,13 +199,16 @@
     shape,
     flow_ref,
     metrics_ref,
+    inv_ref,
     wake_ref,
-    out_ref,
+    state_ref,
+    rate_ref,
     zv,
     relay,
     ym,
     xm,
     wake,
+    inv,
     yv,
     mirror,
     edge,
@@ -228,6 +231,17 @@
     z_low = {"gz": lax.rem(iz + nz - 1, nz)}
     z_high = {"gz": lax.rem(iz + 1, nz)}
 
+    loads = [
+        pltpu.make_async_copy(flow_ref, zv.at[0:5, 3 : 3 + planes], load_sem.at[0]),
+        pltpu.make_async_copy(metrics_ref.at[6:9], zv.at[5:8, 3 : 3 + planes], load_sem.at[1]),
+        pltpu.make_async_copy(metrics_ref.at[0:3], xm, load_sem.at[2]),
+        pltpu.make_async_copy(metrics_ref.at[3:6], ym, load_sem.at[3]),
+        pltpu.make_async_copy(wake_ref, wake, load_sem.at[4]),
+        pltpu.make_async_copy(inv_ref, inv, load_sem.at[5]),
+    ]
+    for copy in loads:
+        copy.start()
+
     barrier = pltpu.get_barrier_semaphore()
 
     def greet(target):
@@ -253,15 +267,8 @@
     other_core = lax.rem(iy, 2) == 1
     when(other_core, lambda: greet(y_low))
 
-    loads = [
-        pltpu.make_async_copy(flow_ref, zv.at[0:5, 3 : 3 + planes], load_sem.at[0]),
-        pltpu.make_async_copy(metrics_ref.at[6:9], zv.at[5:8, 3 : 3 + planes], load_sem.at[1]),
-        pltpu.make_async_copy(metrics_ref.at[0:3], xm, load_sem.at[2]),
-        pltpu.make_async_copy(metrics_ref.at[3:6], ym, load_sem.at[3]),
-        pltpu.make_async_copy(wake_ref, wake, load_sem.at[4]),
-    ]
-    for copy in loads:
-        copy.start()
+    for copy in loads[0:2]:
+        copy.wait()
     as_int = lambda flag: flag.astype(jnp.int32)
     pl.semaphore_wait(
         barrier,
@@ -273,18 +280,6 @@
         + as_int(not_top & jnp.logical_not(other_core)),
     )
 
-    def tell(index, target):
-        pl.semaphore_signal(ready.at[index], inc=1, device_id=target, device_id_type=MESH)
-
-    def hear(index):
-        pl.semaphore_wait(ready.at[index], 1)
-
-    when(not_first, lambda: tell(0, z_low))
-    when(is_last, lambda: tell(1, {"gz": 1}))
-    when(has_left, lambda: tell(2, x_low))
-    when(not_wall, lambda: tell(3, y_low))
-    when(mirror_down, lambda: tell(4, opposite))
-
     lane = lax.broadcasted_iota(jnp.int32, (rows, lanes), 1)
     sublane = lax.broadcasted_iota(jnp.int32, (rows, lanes), 0)
 
@@ -326,9 +321,20 @@
 
         return action
 
-    for copy in loads[0:2]:
-        copy.wait()
     when(is_last & jnp.logical_not(other_core), start(ups))
+
+    def tell(index, target):
+        pl.semaphore_signal(ready.at[index], inc=1, device_id=target, device_id_type=MESH)
+
+    def hear(index):
+        pl.semaphore_wait(ready.at[index], 1)
+
+    when(not_first, lambda: tell(0, z_low))
+    when(is_last, lambda: tell(1, {"gz": 1}))
+    when(has_left, lambda: tell(2, x_low))
+    when(not_wall, lambda: tell(3, y_low))
+    when(mirror_down, lambda: tell(4, opposite))
+
     when(not_first & not_last, start(downs))
     for copy in loads[2:]:
         copy.wait()
@@ -389,7 +395,14 @@
     when(not_wall, start(y_down))
     when(mirror_down, start(to_mirror))
 
+    @pl.when(not_last)
+    def _():
+        hear(0)
+        when(is_first, extra.start)
+        start([ups[2], ups[1], ups[0]])()
+
     def x_plane(p, _):
+        when(is_last & other_core & (p == planes - 1), start(ups))
         flux = lane_sweep([zv[c, 3 + p] for c in range(5)], [xm[j, p] for j in range(3)], 0)
         for c in range(5):
             x_faces[c, p] = flux[c]
@@ -397,14 +410,6 @@
 
     lax.fori_loop(0, planes, x_plane, 0)
 
-    when(is_last & other_core, start(ups))
-
-    @pl.when(not_last)
-    def _():
-        hear(0)
-        when(is_first, extra.start)
-        start([ups[2], ups[1], ups[0]])()
-
     @pl.when(mirror_up)
     def _():
         hear(4)
@@ -423,8 +428,8 @@
     @pl.when(is_second)
     def _():
         extra.wait_recv()
-        for copy in ups:
-            copy.wait_recv()
+        ups[2].wait_recv()
+        ups[1].wait_recv()
         hear(1)
         start(relays)()
 
@@ -483,7 +488,7 @@
         )
     for c in range(5):
         for p in range(planes):
-            out_ref[c, p] = y_parts[c][p]
+            rate_ref[c, p] = y_parts[c][p]
 
     @pl.when(has_left)
     def _():
@@ -520,35 +525,46 @@
             high = pltpu.roll(ends[c], (lanes - 3 - (16 * p + 10)) % lanes, 1)
             upper = jnp.where(lane < 2, low, jnp.where(lane >= lanes - 3, high, x_faces[c, p]))
             lower = pltpu.roll(jnp.where(lane == lanes - 1, low, upper), 1, 1)
-            out_ref[c, p] = out_ref[c, p] + (lower - upper)
+            rate_ref[c, p] = rate_ref[c, p] + (lower - upper)
 
     prepare, one_face = line_steps(zv, terms, faces, 2)
     lax.fori_loop(3, 3 + planes, prepare, 0)
-    for copy in downs:
-        copy.wait_recv()
-    lax.fori_loop(3 + planes, 6 + planes, prepare, 0)
+    below_last = 2 * iz < nz
+    pick = lambda low, high: jnp.where(below_last, low, high)
+
+    def arrival(slot, index):
+        return remote(zv.at[:, 3], zv.at[:, slot], index, z_high)
 
     def finish(k, _):
+        volume = inv[k]
         for c in range(5):
-            out_ref[c, k] = out_ref[c, k] + (faces[c, k] - faces[c, k + 1])
+            rate = volume * (rate_ref[c, k] + (faces[c, k] - faces[c, k + 1]))
+            rate_ref[c, k] = rate
+            state_ref[c, k] = zv[c, 3 + k] + STEP_SIZE * rate
         return _
 
-    lax.fori_loop(3, planes + 1, one_face, 0)
-    lax.fori_loop(3, planes, finish, 0)
-
-    def near_face(j, carry):
-        k = 2 - j
-
-        @pl.when(jnp.logical_not(is_second))
+    def soon(j, carry):
+        slot = pick(7 + j, 2 - j)
+        arrival(slot, pick(Z_DOWN + j, Z_UP + j)).wait_recv()
+        return prepare(slot, carry)
+
+    lax.fori_loop(0, 3, soon, 0)
+    lax.fori_loop(0, 2, lambda j, carry: one_face(pick(3 + j, j), carry), 0)
+    finish(pick(3, 0), 0)
+
+    def late(j, carry):
+        slot = pick(2 - j, 7 + j)
+
+        @pl.when(jnp.logical_not(is_second) | (j == 0))
         def _():
-            up_copy(j).wait_recv()
-
-        prepare(k, 0)
-        one_face(k, 0)
-        finish(k, 0)
+            arrival(slot, pick(Z_UP + j, Z_DOWN + j)).wait_recv()
+
+        prepare(slot, 0)
+        one_face(pick(2 - j, 2 + j), 0)
+        finish(pick(2 - j, 1 + j), 0)
         return carry
 
-    lax.fori_loop(0, 3, near_face, 0)
+    lax.fori_loop(0, 3, late, 0)
 
     for copy in ups:
         copy.wait_send()
@@ -589,6 +605,17 @@
     def _():
         for copy in y_up:
             copy.wait_send()
+
+
+def store(state_ref, rate_ref, state_out, rate_out, sem):
+    copies = [
+        pltpu.make_async_copy(state_ref, state_out, sem.at[0]),
+        pltpu.make_async_copy(rate_ref, rate_out, sem.at[1]),
+    ]
+    for copy in copies:
+        copy.start()
+    for copy in copies:
+        copy.wait()
 
 
 def solution(mesh):
@@ -597,18 +624,19 @@
     def local(conserved, metrics, inv_volume, wake_donor):
         planes, rows, lanes = conserved.shape[1:]
         tile = (rows, lanes)
-        operands = (conserved, metrics, wake_donor.reshape(1, lanes))
-        summed = pl.pallas_call(
+        operands = (conserved, metrics, inv_volume, wake_donor.reshape(1, lanes))
+        results = pl.pallas_call(
             functools.partial(kernel, (nx, ny, nz)),
-            out_shape=jax.ShapeDtypeStruct(conserved.shape, F32),
-            in_specs=[pl.BlockSpec(memory_space=pltpu.HBM)] * 3,
-            out_specs=pl.BlockSpec(memory_space=pltpu.VMEM),
+            out_shape=[jax.ShapeDtypeStruct(conserved.shape, F32)] * 2,
+            in_specs=[pl.BlockSpec(memory_space=pltpu.HBM)] * 4,
+            out_specs=[pl.BlockSpec(memory_space=pltpu.VMEM)] * 2,
             scratch_shapes=[
                 pltpu.VMEM((8, planes + 6) + tile, F32),
                 pltpu.VMEM((8,) + tile, F32),
                 pltpu.VMEM((3, planes) + tile, F32),
                 pltpu.VMEM((3, planes) + tile, F32),
                 pltpu.VMEM((1, lanes), jnp.int32),
+                pltpu.VMEM((planes,) + tile, F32),
                 pltpu.VMEM((8, 10) + tile, F32),
                 pltpu.VMEM((8, 3) + tile, F32),
                 pltpu.VMEM((8,) + tile, F32),
@@ -618,7 +646,7 @@
                 pltpu.VMEM((5, 5) + tile, F32),
                 pltpu.VMEM((5, planes) + tile, F32),
                 pltpu.SemaphoreType.REGULAR((5,)),
-                pltpu.SemaphoreType.DMA((5,)),
+                pltpu.SemaphoreType.DMA((6,)),
                 pltpu.SemaphoreType.DMA((2 * N_SEMS,)),
                 pltpu.SemaphoreType.DMA((2 * N_SEMS,)),
             ],
@@ -629,8 +657,14 @@
                 flops=60_000_000, bytes_accessed=500_000, transcendentals=0
             ),
         )(*[pltpu.with_memory_space_constraint(x, pltpu.HBM) for x in operands])
-        time_rate = inv_volume[None] * summed
-        return (conserved + STEP_SIZE * time_rate, time_rate)
+        return pl.pallas_call(
+            store,
+            out_shape=[jax.ShapeDtypeStruct(conserved.shape, F32)] * 2,
+            in_specs=[pl.BlockSpec(memory_space=pltpu.VMEM)] * 2,
+            out_specs=[pl.BlockSpec(memory_space=pltpu.HBM)] * 2,
+            scratch_shapes=[pltpu.SemaphoreType.DMA((2,))],
+            compiler_params=pltpu.CompilerParams(vmem_limit_bytes=1024 * 1024),
+        )(*results)
 
     placed = (P(None, "gz", "gy", "gx"), P(None, "gz", "gy", "gx"), P("gz", "gy", "gx"), P("gx"))
     return jax.shard_map(

time: 12.5 us -> 12 us (0.960)
  the two profiles are of different devices: /device:TPU:28 before, /device:TPU:0 now
where the time goes in v3:
time: 12 us; the launch traced here: 11.8 us
  Pallas kernels  11.2 us (93%)
  between operations  0.64 us (5%)
    pallas_call x1, Pallas kernels, local(): pl.pallas_call(functools.partial(kernel, (nx, ny, nz)), out_shape=[jax.Sh...  10.5 us
    pallas_call x1, Pallas kernels, local(): pl.pallas_call(store, out_shape=[jax.ShapeDtypeStruct(conserved.shape, F3...  0.68 us

profile of v3, /device:TPU:0, one launch (start us, length us, event | category | flops | bytes accessed | tf_op | source)
XLA Modules:
  0.0 11.8 jit_solution(5098865731478042853)
XLA Ops:
  0.6 10.5 %shard_map.59 = (f32[5,4,8,128]{3,2,1,0:T(8,128)S(1)}, f32[5,4,8,128]{3,2,1,0:T(8,128)S(1)}) custom-call(f32[5,4,8,128]{3,2,1,0:T(8,128)} %flow_ref.1, f32[9,4,8,128]{3,2,1,0:T(8,128)} %metrics_ref.1, f32[4,8,128]{2,1,0:T(8,128)} %inv_ref.1, s32[1,128]{1,0:T(1,128)} %bitcast.1), custom_call_target="tpu_custom_call" | custom-call | flops 60000000 | bytes 500000 | tf_op jit(solution)/shard_map/pallas_call | solution.py:628
  11.1 0.7 %shard_map.60 = (f32[5,4,8,128]{3,2,1,0:T(8,128)}, f32[5,4,8,128]{3,2,1,0:T(8,128)}) custom-call(f32[5,4,8,128]{3,2,1,0:T(8,128)S(1)} %get-tuple-element.4.state_ref, f32[5,4,8,128]{3,2,1,0:T(8,128)S(1)} %get-tuple-element.5.rate_ref), custom_call_target="tpu_custom_call" | custom-call | tf_op jit(solution)/shard_map/pallas_call | solution.py:660

commit v4 on v3

--- a/solution.py
+++ b/solution.py
@@ -216,6 +216,8 @@
     edge_high,
     terms,
     faces,
+    z_terms,
+    z_faces,
     x_faces,
     ready,
     load_sem,
@@ -231,6 +233,111 @@
     z_low = {"gz": lax.rem(iz + nz - 1, nz)}
     z_high = {"gz": lax.rem(iz + 1, nz)}
 
+    barrier = pltpu.get_barrier_semaphore()
+
+    def greet(target):
+        pl.semaphore_signal(barrier, inc=1, device_id=target, device_id_type=MESH)
+
+    is_first, is_second, is_last = iz == 0, iz == 1, iz == nz - 1
+    mirror_up = at_wall & (partner > ix)
+    mirror_down = at_wall & (partner < ix)
+    not_first, not_last = jnp.logical_not(is_first), jnp.logical_not(is_last)
+    not_wall, not_top = jnp.logical_not(at_wall), jnp.logical_not(at_top)
+    x_low, x_high = {"gx": ix - 1}, {"gx": ix + 1}
+    y_low, y_high = {"gy": iy - 1}, {"gy": iy + 1}
+    opposite = {"gx": partner}
+
+    def when(condition, action):
+        pl.when(condition)(action)
+
+    when(not_last, lambda: greet(z_high))
+    when(is_first | is_second, lambda: greet({"gz": nz - 1}))
+    when(has_right, lambda: greet(x_high))
+    when(not_top, lambda: greet(y_high))
+    when(mirror_up, lambda: greet(opposite))
+    other_core = lax.rem(iy, 2) == 1
+    when(other_core, lambda: greet(y_low))
+
+    as_int = lambda flag: flag.astype(jnp.int32)
+    pl.semaphore_wait(
+        barrier,
+        as_int(not_first)
+        + 2 * as_int(is_last)
+        + as_int(has_left)
+        + as_int(not_wall)
+        + as_int(mirror_down)
+        + as_int(not_top & jnp.logical_not(other_core)),
+    )
+
+    lane = lax.broadcasted_iota(jnp.int32, (rows, lanes), 1)
+    sublane = lax.broadcasted_iota(jnp.int32, (rows, lanes), 0)
+
+    def remote(src, dst, index, target):
+        return pltpu.make_async_remote_copy(
+            src_ref=src,
+            dst_ref=dst,
+            send_sem=send_sem.at[index],
+            recv_sem=recv_sem.at[index],
+            device_id=target,
+            device_id_type=MESH,
+        )
+
+    def up_copy(j):
+        return remote(zv.at[:, 2 + planes - j], zv.at[:, 2 - j], Z_UP + j, z_high)
+
+    def down_copy(j):
+        return remote(zv.at[:, 3 + j], zv.at[:, 3 + planes + j], Z_DOWN + j, z_low)
+
+    def relay_copy(j):
+        return pltpu.make_async_remote_copy(
+            src_ref=relay if j == 0 else zv.at[:, j - 1],
+            dst_ref=zv.at[:, 3 + planes + j],
+            send_sem=send_sem.at[RELAY + j],
+            recv_sem=recv_sem.at[Z_DOWN + j],
+            device_id={"gz": nz - 1},
+            device_id_type=MESH,
+        )
+
+    extra = remote(zv.at[:, 3], relay, Z_LAST, z_high)
+    ups = [up_copy(j) for j in range(3)]
+    downs = [down_copy(j) for j in range(3)]
+    relays = [relay_copy(j) for j in range(3)]
+
+    def start(copies):
+        def action():
+            for copy in copies:
+                copy.start()
+
+        return action
+
+    def start_wrap():
+        for j in range(3):
+            plane = planes - 1 - j
+            for part, low, high in ((flow_ref.at[:, plane], 0, 5), (metrics_ref.at[6:9, plane], 5, 8)):
+                pltpu.make_async_remote_copy(
+                    src_ref=part,
+                    dst_ref=zv.at[low:high, 2 - j],
+                    send_sem=send_sem.at[Z_UP + j],
+                    recv_sem=recv_sem.at[Z_UP + j],
+                    device_id=z_high,
+                    device_id_type=MESH,
+                ).start()
+
+    when(is_last, start_wrap)
+
+    def start_downs():
+        for j in range(3):
+            for part, low, high in ((flow_ref.at[:, j], 0, 5), (metrics_ref.at[6:9, j], 5, 8)):
+                pltpu.make_async_remote_copy(
+                    src_ref=part,
+                    dst_ref=zv.at[low:high, 3 + planes + j],
+                    send_sem=send_sem.at[Z_DOWN + j],
+                    recv_sem=recv_sem.at[Z_DOWN + j],
+                    device_id=z_low,
+                    device_id_type=MESH,
+                ).start()
+
+    when(not_first & not_last, start_downs)
     loads = [
         pltpu.make_async_copy(flow_ref, zv.at[0:5, 3 : 3 + planes], load_sem.at[0]),
         pltpu.make_async_copy(metrics_ref.at[6:9], zv.at[5:8, 3 : 3 + planes], load_sem.at[1]),
@@ -242,87 +349,6 @@
     for copy in loads:
         copy.start()
 
-    barrier = pltpu.get_barrier_semaphore()
-
-    def greet(target):
-        pl.semaphore_signal(barrier, inc=1, device_id=target, device_id_type=MESH)
-
-    is_first, is_second, is_last = iz == 0, iz == 1, iz == nz - 1
-    mirror_up = at_wall & (partner > ix)
-    mirror_down = at_wall & (partner < ix)
-    not_first, not_last = jnp.logical_not(is_first), jnp.logical_not(is_last)
-    not_wall, not_top = jnp.logical_not(at_wall), jnp.logical_not(at_top)
-    x_low, x_high = {"gx": ix - 1}, {"gx": ix + 1}
-    y_low, y_high = {"gy": iy - 1}, {"gy": iy + 1}
-    opposite = {"gx": partner}
-
-    def when(condition, action):
-        pl.when(condition)(action)
-
-    when(not_last, lambda: greet(z_high))
-    when(is_first | is_second, lambda: greet({"gz": nz - 1}))
-    when(has_right, lambda: greet(x_high))
-    when(not_top, lambda: greet(y_high))
-    when(mirror_up, lambda: greet(opposite))
-    other_core = lax.rem(iy, 2) == 1
-    when(other_core, lambda: greet(y_low))
-
-    for copy in loads[0:2]:
-        copy.wait()
-    as_int = lambda flag: flag.astype(jnp.int32)
-    pl.semaphore_wait(
-        barrier,
-        as_int(not_first)
-        + 2 * as_int(is_last)
-        + as_int(has_left)
-        + as_int(not_wall)
-        + as_int(mirror_down)
-        + as_int(not_top & jnp.logical_not(other_core)),
-    )
-
-    lane = lax.broadcasted_iota(jnp.int32, (rows, lanes), 1)
-    sublane = lax.broadcasted_iota(jnp.int32, (rows, lanes), 0)
-
-    def remote(src, dst, index, target):
-        return pltpu.make_async_remote_copy(
-            src_ref=src,
-            dst_ref=dst,
-            send_sem=send_sem.at[index],
-            recv_sem=recv_sem.at[index],
-            device_id=target,
-            device_id_type=MESH,
-        )
-
-    def up_copy(j):
-        return remote(zv.at[:, 2 + planes - j], zv.at[:, 2 - j], Z_UP + j, z_high)
-
-    def down_copy(j):
-        return remote(zv.at[:, 3 + j], zv.at[:, 3 + planes + j], Z_DOWN + j, z_low)
-
-    def relay_copy(j):
-        return pltpu.make_async_remote_copy(
-            src_ref=relay if j == 0 else zv.at[:, j - 1],
-            dst_ref=zv.at[:, 3 + planes + j],
-            send_sem=send_sem.at[RELAY + j],
-            recv_sem=recv_sem.at[Z_DOWN + j],
-            device_id={"gz": nz - 1},
-            device_id_type=MESH,
-        )
-
-    extra = remote(zv.at[:, 3], relay, Z_LAST, z_high)
-    ups = [up_copy(j) for j in range(3)]
-    downs = [down_copy(j) for j in range(3)]
-    relays = [relay_copy(j) for j in range(3)]
-
-    def start(copies):
-        def action():
-            for copy in copies:
-                copy.start()
-
-        return action
-
-    when(is_last & jnp.logical_not(other_core), start(ups))
-
     def tell(index, target):
         pl.semaphore_signal(ready.at[index], inc=1, device_id=target, device_id_type=MESH)
 
@@ -335,7 +361,8 @@
     when(not_wall, lambda: tell(3, y_low))
     when(mirror_down, lambda: tell(4, opposite))
 
-    when(not_first & not_last, start(downs))
+    for copy in loads[0:2]:
+        copy.wait()
     for copy in loads[2:]:
         copy.wait()
 
@@ -401,8 +428,22 @@
         when(is_first, extra.start)
         start([ups[2], ups[1], ups[0]])()
 
+    @pl.when(mirror_up)
+    def _():
+        hear(4)
+        start(to_mirror)()
+
+    @pl.when(not_top)
+    def _():
+        hear(3)
+        start(y_up)()
+
+    @pl.when(has_right)
+    def _():
+        hear(2)
+        x_up.start()
+
     def x_plane(p, _):
-        when(is_last & other_core & (p == planes - 1), start(ups))
         flux = lane_sweep([zv[c, 3 + p] for c in range(5)], [xm[j, p] for j in range(3)], 0)
         for c in range(5):
             x_faces[c, p] = flux[c]
@@ -410,28 +451,12 @@
 
     lax.fori_loop(0, planes, x_plane, 0)
 
-    @pl.when(mirror_up)
-    def _():
-        hear(4)
-        start(to_mirror)()
-
-    @pl.when(not_top)
-    def _():
-        hear(3)
-        start(y_up)()
-
-    @pl.when(has_right)
-    def _():
-        hear(2)
-        x_up.start()
-
     @pl.when(is_second)
     def _():
-        extra.wait_recv()
-        ups[2].wait_recv()
-        ups[1].wait_recv()
         hear(1)
-        start(relays)()
+        for arriving, leaving in zip((extra, ups[2], ups[1]), relays):
+            arriving.wait_recv()
+            leaving.start()
 
     when(is_last, start(downs))
 
@@ -446,6 +471,11 @@
             yv[c, k, 4:8] = swapped[1 + k][0:4]
             yv[c, 7 + k, 0:4] = swapped[k][4:8]
 
+    prepare_y, face_y = line_steps(yv, terms, faces, 1)
+    prepare_z, face_z = line_steps(zv, z_terms, z_faces, 2)
+    lax.fori_loop(3, 3 + planes, prepare_z, 0)
+    lax.fori_loop(3, 7, prepare_y, 0)
+
     @pl.when(jnp.logical_not(at_top))
     def _():
         for copy in y_down:
@@ -456,6 +486,9 @@
         for c in range(8):
             for k in range(3):
                 yv[c, 7 + k, 4:8] = yv[c, 6, 4:8]
+
+    lax.fori_loop(7, 10, prepare_y, 0)
+    lax.fori_loop(3, 5, face_y, 0)
 
     @pl.when(jnp.logical_not(at_wall))
     def _():
@@ -478,9 +511,8 @@
                     here = -here
                 yv[c, 2 - k, 0:4] = jnp.where(is_wake, facing, here)[0:4]
 
-    prepare, one_face = line_steps(yv, terms, faces, 1)
-    lax.fori_loop(0, 10, prepare, 0)
-    lax.fori_loop(0, 5, one_face, 0)
+    lax.fori_loop(0, 3, prepare_y, 0)
+    lax.fori_loop(0, 3, face_y, 0)
     y_parts = []
     for c in range(5):
         y_parts.append(
@@ -527,8 +559,6 @@
             lower = pltpu.roll(jnp.where(lane == lanes - 1, low, upper), 1, 1)
             rate_ref[c, p] = rate_ref[c, p] + (lower - upper)
 
-    prepare, one_face = line_steps(zv, terms, faces, 2)
-    lax.fori_loop(3, 3 + planes, prepare, 0)
     below_last = 2 * iz < nz
     pick = lambda low, high: jnp.where(below_last, low, high)
 
@@ -538,7 +568,7 @@
     def finish(k, _):
         volume = inv[k]
         for c in range(5):
-            rate = volume * (rate_ref[c, k] + (faces[c, k] - faces[c, k + 1]))
+            rate = volume * (rate_ref[c, k] + (z_faces[c, k] - z_faces[c, k + 1]))
             rate_ref[c, k] = rate
             state_ref[c, k] = zv[c, 3 + k] + STEP_SIZE * rate
         return _
@@ -546,10 +576,10 @@
     def soon(j, carry):
         slot = pick(7 + j, 2 - j)
         arrival(slot, pick(Z_DOWN + j, Z_UP + j)).wait_recv()
-        return prepare(slot, carry)
+        return prepare_z(slot, carry)
 
     lax.fori_loop(0, 3, soon, 0)
-    lax.fori_loop(0, 2, lambda j, carry: one_face(pick(3 + j, j), carry), 0)
+    lax.fori_loop(0, 2, lambda j, carry: face_z(pick(3 + j, j), carry), 0)
     finish(pick(3, 0), 0)
 
     def late(j, carry):
@@ -559,13 +589,11 @@
         def _():
             arrival(slot, pick(Z_UP + j, Z_DOWN + j)).wait_recv()
 
-        prepare(slot, 0)
-        one_face(pick(2 - j, 2 + j), 0)
+        prepare_z(slot, 0)
+        face_z(pick(2 - j, 2 + j), 0)
         finish(pick(2 - j, 1 + j), 0)
         return carry
 
-    lax.fori_loop(0, 3, late, 0)
-
     for copy in ups:
         copy.wait_send()
 
@@ -578,11 +606,6 @@
         for copy in downs:
             copy.wait_send()
 
-    @pl.when(is_second)
-    def _():
-        for copy in relays:
-            copy.wait_send()
-
     @pl.when(has_left)
     def _():
         x_down.wait_send()
@@ -604,6 +627,13 @@
     @pl.when(jnp.logical_not(at_top))
     def _():
         for copy in y_up:
+            copy.wait_send()
+
+    lax.fori_loop(0, 3, late, 0)
+
+    @pl.when(is_second)
+    def _():
+        for copy in relays:
             copy.wait_send()
 
 
@@ -644,6 +674,8 @@
                 pltpu.VMEM((8,) + tile, F32),
                 pltpu.VMEM((10, 10) + tile, F32),
                 pltpu.VMEM((5, 5) + tile, F32),
+                pltpu.VMEM((10, planes + 6) + tile, F32),
+                pltpu.VMEM((5, planes + 1) + tile, F32),
                 pltpu.VMEM((5, planes) + tile, F32),
                 pltpu.SemaphoreType.REGULAR((5,)),
                 pltpu.SemaphoreType.DMA((6,)),

time: 12 us -> 11.4 us (0.950)
  Pallas kernels: 11.2 us -> 10.6 us
    pallas_call x1, Pallas kernels: 10.5 us -> 9.94 us  [local(): pl.pallas_call(functools.partial(kernel, (nx, ny, nz)), out_shape=[jax.Sh...]
where the time goes in v4:
time: 11.4 us; the launch traced here: 11.3 us
  Pallas kernels  10.6 us (93%)
  between operations  0.64 us (6%)
    pallas_call x1, Pallas kernels, local(): pl.pallas_call(functools.partial(kernel, (nx, ny, nz)), out_shape=[jax.Sh...  9.94 us
    pallas_call x1, Pallas kernels, local(): pl.pallas_call(store, out_shape=[jax.ShapeDtypeStruct(conserved.shape, F3...  0.68 us

profile of v4, /device:TPU:0, one launch (start us, length us, event | category | flops | bytes accessed | tf_op | source)
XLA Modules:
  0.0 11.3 jit_solution(9480163764492037338)
XLA Ops:
  0.6 9.9 %shard_map.59 = (f32[5,4,8,128]{3,2,1,0:T(8,128)S(1)}, f32[5,4,8,128]{3,2,1,0:T(8,128)S(1)}) custom-call(f32[5,4,8,128]{3,2,1,0:T(8,128)} %flow_ref.1, f32[9,4,8,128]{3,2,1,0:T(8,128)} %metrics_ref.1, f32[4,8,128]{2,1,0:T(8,128)} %inv_ref.1, s32[1,128]{1,0:T(1,128)} %bitcast.1), custom_call_target="tpu_custom_call" | custom-call | flops 60000000 | bytes 500000 | tf_op jit(solution)/shard_map/pallas_call | solution.py:658
  10.6 0.7 %shard_map.60 = (f32[5,4,8,128]{3,2,1,0:T(8,128)}, f32[5,4,8,128]{3,2,1,0:T(8,128)}) custom-call(f32[5,4,8,128]{3,2,1,0:T(8,128)S(1)} %get-tuple-element.4.state_ref, f32[5,4,8,128]{3,2,1,0:T(8,128)S(1)} %get-tuple-element.5.rate_ref), custom_call_target="tpu_custom_call" | custom-call | tf_op jit(solution)/shard_map/pallas_call | solution.py:692

commit v5 on v4

--- a/solution.py
+++ b/solution.py
@@ -310,8 +310,8 @@
 
         return action
 
-    def start_wrap():
-        for j in range(3):
+    def start_wrap(count):
+        for j in count:
             plane = planes - 1 - j
             for part, low, high in ((flow_ref.at[:, plane], 0, 5), (metrics_ref.at[6:9, plane], 5, 8)):
                 pltpu.make_async_remote_copy(
@@ -323,7 +323,8 @@
                     device_id_type=MESH,
                 ).start()
 
-    when(is_last, start_wrap)
+    when(is_last, lambda: start_wrap((0,)))
+    when(is_last & jnp.logical_not(other_core), lambda: start_wrap((1, 2)))
 
     def start_downs():
         for j in range(3):
@@ -337,53 +338,9 @@
                     device_id_type=MESH,
                 ).start()
 
-    when(not_first & not_last, start_downs)
-    loads = [
-        pltpu.make_async_copy(flow_ref, zv.at[0:5, 3 : 3 + planes], load_sem.at[0]),
-        pltpu.make_async_copy(metrics_ref.at[6:9], zv.at[5:8, 3 : 3 + planes], load_sem.at[1]),
-        pltpu.make_async_copy(metrics_ref.at[0:3], xm, load_sem.at[2]),
-        pltpu.make_async_copy(metrics_ref.at[3:6], ym, load_sem.at[3]),
-        pltpu.make_async_copy(wake_ref, wake, load_sem.at[4]),
-        pltpu.make_async_copy(inv_ref, inv, load_sem.at[5]),
-    ]
-    for copy in loads:
-        copy.start()
-
-    def tell(index, target):
-        pl.semaphore_signal(ready.at[index], inc=1, device_id=target, device_id_type=MESH)
-
-    def hear(index):
-        pl.semaphore_wait(ready.at[index], 1)
-
-    when(not_first, lambda: tell(0, z_low))
-    when(is_last, lambda: tell(1, {"gz": 1}))
-    when(has_left, lambda: tell(2, x_low))
-    when(not_wall, lambda: tell(3, y_low))
-    when(mirror_down, lambda: tell(4, opposite))
-
-    for copy in loads[0:2]:
-        copy.wait()
-    for copy in loads[2:]:
-        copy.wait()
-
-    def source(c, p):
-        return zv[c, 3 + p] if c < 5 else xm[c - 5, p]
-
-    for c in range(8):
-        packed = source(c, planes - 1)
-        for p in range(planes):
-            value = source(c, p)
-            low = pltpu.roll(value, 16 * p + 3, 1)
-            high = pltpu.roll(value, (16 * p + 13) % lanes, 1)
-            packed = jnp.where((lane >= 16 * p + 3) & (lane < 16 * p + 8), low, packed)
-            packed = jnp.where((lane >= 16 * p + 8) & (lane < 16 * p + 13), high, packed)
-        edge[c] = packed
-
-    x_down = remote(edge, edge_high, X_DOWN, x_low)
-    x_up = remote(edge, edge_low, X_UP, x_high)
-    when(has_left, x_down.start)
-
-    def y_copies(kind):
+    def y_copies(kind, early):
+        flow = flow_ref if early else zv.at[0:5, 3 : 3 + planes]
+        row = metrics_ref.at[3:6] if early else ym
         copies = []
         for j in range(3):
             if kind == "down":
@@ -397,7 +354,7 @@
                 flow_dst = lambda lo, hi: mirror.at[lo:hi, j, 0:4, :]
             copies.append(
                 pltpu.make_async_remote_copy(
-                    src_ref=zv.at[0:5, 3 : 3 + planes, cell, :],
+                    src_ref=flow.at[:, :, cell, :],
                     dst_ref=flow_dst(0, 5),
                     send_sem=send_sem.at[index],
                     recv_sem=recv_sem.at[index],
@@ -407,7 +364,7 @@
             )
             copies.append(
                 pltpu.make_async_remote_copy(
-                    src_ref=ym.at[:, :, cell, :],
+                    src_ref=row.at[:, :, cell, :],
                     dst_ref=flow_dst(5, 8),
                     send_sem=send_sem.at[N_SEMS + index],
                     recv_sem=recv_sem.at[N_SEMS + index],
@@ -417,10 +374,56 @@
             )
         return copies
 
-    y_down, y_up, to_mirror = y_copies("down"), y_copies("up"), y_copies("mirror")
-
+    y_down, y_up = y_copies("down", True), y_copies("up", False)
+    to_mirror = y_copies("mirror", False)
+
+    when(not_first & not_last, start_downs)
+    when(mirror_down, start(y_copies("mirror", True)))
     when(not_wall, start(y_down))
-    when(mirror_down, start(to_mirror))
+    loads = [
+        pltpu.make_async_copy(flow_ref, zv.at[0:5, 3 : 3 + planes], load_sem.at[0]),
+        pltpu.make_async_copy(metrics_ref.at[6:9], zv.at[5:8, 3 : 3 + planes], load_sem.at[1]),
+        pltpu.make_async_copy(metrics_ref.at[0:3], xm, load_sem.at[2]),
+        pltpu.make_async_copy(metrics_ref.at[3:6], ym, load_sem.at[3]),
+        pltpu.make_async_copy(wake_ref, wake, load_sem.at[4]),
+        pltpu.make_async_copy(inv_ref, inv, load_sem.at[5]),
+    ]
+    for copy in loads:
+        copy.start()
+
+    def tell(index, target):
+        pl.semaphore_signal(ready.at[index], inc=1, device_id=target, device_id_type=MESH)
+
+    def hear(index):
+        pl.semaphore_wait(ready.at[index], 1)
+
+    when(not_first, lambda: tell(0, z_low))
+    when(is_last, lambda: tell(1, {"gz": 1}))
+    when(has_left, lambda: tell(2, x_low))
+    when(not_wall, lambda: tell(3, y_low))
+    when(mirror_down, lambda: tell(4, opposite))
+
+    for copy in loads[0:2]:
+        copy.wait()
+    for copy in loads[2:]:
+        copy.wait()
+
+    def source(c, p):
+        return zv[c, 3 + p] if c < 5 else xm[c - 5, p]
+
+    for c in range(8):
+        packed = source(c, planes - 1)
+        for p in range(planes):
+            value = source(c, p)
+            low = pltpu.roll(value, 16 * p + 3, 1)
+            high = pltpu.roll(value, (16 * p + 13) % lanes, 1)
+            packed = jnp.where((lane >= 16 * p + 3) & (lane < 16 * p + 8), low, packed)
+            packed = jnp.where((lane >= 16 * p + 8) & (lane < 16 * p + 13), high, packed)
+        edge[c] = packed
+
+    x_down = remote(edge, edge_high, X_DOWN, x_low)
+    x_up = remote(edge, edge_low, X_UP, x_high)
+    when(has_left, x_down.start)
 
     @pl.when(not_last)
     def _():
@@ -444,6 +447,7 @@
         x_up.start()
 
     def x_plane(p, _):
+        when(is_last & other_core & (p == 1), start(ups[1:]))
         flux = lane_sweep([zv[c, 3 + p] for c in range(5)], [xm[j, p] for j in range(3)], 0)
         for c in range(5):
             x_faces[c, p] = flux[c]

time: 11.4 us -> 10.9 us (0.956)
  Pallas kernels: 10.6 us -> 10.1 us
    pallas_call x1, Pallas kernels: 9.94 us -> 9.4 us  [local(): pl.pallas_call(functools.partial(kernel, (nx, ny, nz)), out_shape=[jax.Sh...]
where the time goes in v5:
time: 10.9 us; the launch traced here: 10.7 us
  Pallas kernels  10.1 us (93%)
  between operations  0.64 us (6%)
    pallas_call x1, Pallas kernels, local(): pl.pallas_call(functools.partial(kernel, (nx, ny, nz)), out_shape=[jax.Sh...  9.4 us
    pallas_call x1, Pallas kernels, local(): pl.pallas_call(store, out_shape=[jax.ShapeDtypeStruct(conserved.shape, F3...  0.68 us

profile of v5, /device:TPU:0, one launch (start us, length us, event | category | flops | bytes accessed | tf_op | source)
XLA Modules:
  0.0 10.7 jit_solution(17823451255072606256)
XLA Ops:
  0.6 9.4 %shard_map.59 = (f32[5,4,8,128]{3,2,1,0:T(8,128)S(1)}, f32[5,4,8,128]{3,2,1,0:T(8,128)S(1)}) custom-call(f32[5,4,8,128]{3,2,1,0:T(8,128)} %flow_ref.1, f32[9,4,8,128]{3,2,1,0:T(8,128)} %metrics_ref.1, f32[4,8,128]{2,1,0:T(8,128)} %inv_ref.1, s32[1,128]{1,0:T(1,128)} %bitcast.1), custom_call_target="tpu_custom_call" | custom-call | flops 60000000 | bytes 500000 | tf_op jit(solution)/shard_map/pallas_call | solution.py:662
  10.0 0.7 %shard_map.60 = (f32[5,4,8,128]{3,2,1,0:T(8,128)}, f32[5,4,8,128]{3,2,1,0:T(8,128)}) custom-call(f32[5,4,8,128]{3,2,1,0:T(8,128)S(1)} %get-tuple-element.4.state_ref, f32[5,4,8,128]{3,2,1,0:T(8,128)S(1)} %get-tuple-element.5.rate_ref), custom_call_target="tpu_custom_call" | custom-call | tf_op jit(solution)/shard_map/pallas_call | solution.py:696

commit v6 on v5

--- a/solution.py
+++ b/solution.py
@@ -447,7 +447,8 @@
         x_up.start()
 
     def x_plane(p, _):
-        when(is_last & other_core & (p == 1), start(ups[1:]))
+        when(is_last & other_core & (p == 1), start(ups[1:2]))
+        when(is_last & other_core & (p == 2), start(ups[2:]))
         flux = lane_sweep([zv[c, 3 + p] for c in range(5)], [xm[j, p] for j in range(3)], 0)
         for c in range(5):
             x_faces[c, p] = flux[c]
@@ -654,6 +655,7 @@
 
 def solution(mesh):
     nx, ny, nz = mesh.shape["gx"], mesh.shape["gy"], mesh.shape["gz"]
+    assert nz > 2 and nx % 2 == 0
 
     def local(conserved, metrics, inv_volume, wake_donor):
         planes, rows, lanes = conserved.shape[1:]

time: 10.9 us -> 10.9 us (level)
  no operation moved by 1% of the time
where the time goes in v6:
time: 10.9 us; the launch traced here: 10.7 us
  Pallas kernels  10.1 us (93%)
  between operations  0.64 us (6%)
    pallas_call x1, Pallas kernels, local(): pl.pallas_call(functools.partial(kernel, (nx, ny, nz)), out_shape=[jax.Sh...  9.4 us
    pallas_call x1, Pallas kernels, local(): pl.pallas_call(store, out_shape=[jax.ShapeDtypeStruct(conserved.shape, F3...  0.68 us

profile of v6, /device:TPU:0, one launch (start us, length us, event | category | flops | bytes accessed | tf_op | source)
XLA Modules:
  0.0 10.7 jit_solution(5253250769560767756)
XLA Ops:
  0.6 9.4 %shard_map.59 = (f32[5,4,8,128]{3,2,1,0:T(8,128)S(1)}, f32[5,4,8,128]{3,2,1,0:T(8,128)S(1)}) custom-call(f32[5,4,8,128]{3,2,1,0:T(8,128)} %flow_ref.1, f32[9,4,8,128]{3,2,1,0:T(8,128)} %metrics_ref.1, f32[4,8,128]{2,1,0:T(8,128)} %inv_ref.1, s32[1,128]{1,0:T(1,128)} %bitcast.1), custom_call_target="tpu_custom_call" | custom-call | flops 60000000 | bytes 500000 | tf_op jit(solution)/shard_map/pallas_call | solution.py:664
  10.0 0.7 %shard_map.60 = (f32[5,4,8,128]{3,2,1,0:T(8,128)}, f32[5,4,8,128]{3,2,1,0:T(8,128)}) custom-call(f32[5,4,8,128]{3,2,1,0:T(8,128)S(1)} %get-tuple-element.4.state_ref, f32[5,4,8,128]{3,2,1,0:T(8,128)S(1)} %get-tuple-element.5.rate_ref), custom_call_target="tpu_custom_call" | custom-call | tf_op jit(solution)/shard_map/pallas_call | solution.py:698

commit v7 on v5

--- a/solution.py
+++ b/solution.py
@@ -429,7 +429,8 @@
     def _():
         hear(0)
         when(is_first, extra.start)
-        start([ups[2], ups[1], ups[0]])()
+        start([ups[2], ups[1]])()
+        when(not_first, ups[0].start)
 
     @pl.when(mirror_up)
     def _():
@@ -454,6 +455,7 @@
         return _
 
     lax.fori_loop(0, planes, x_plane, 0)
+    when(is_first, ups[0].start)
 
     @pl.when(is_second)
     def _():

time: 10.9 us -> 10.9 us (level)
  no operation moved by 1% of the time
where the time goes in v7:
time: 10.9 us; the launch traced here: 10.7 us
  Pallas kernels  10.1 us (93%)
  between operations  0.64 us (6%)
    pallas_call x1, Pallas kernels, local(): pl.pallas_call(functools.partial(kernel, (nx, ny, nz)), out_shape=[jax.Sh...  9.4 us
    pallas_call x1, Pallas kernels, local(): pl.pallas_call(store, out_shape=[jax.ShapeDtypeStruct(conserved.shape, F3...  0.68 us

profile of v7, /device:TPU:0, one launch (start us, length us, event | category | flops | bytes accessed | tf_op | source)
XLA Modules:
  0.0 10.7 jit_solution(9403717726070065282)
XLA Ops:
  0.6 9.4 %shard_map.59 = (f32[5,4,8,128]{3,2,1,0:T(8,128)S(1)}, f32[5,4,8,128]{3,2,1,0:T(8,128)S(1)}) custom-call(f32[5,4,8,128]{3,2,1,0:T(8,128)} %flow_ref.1, f32[9,4,8,128]{3,2,1,0:T(8,128)} %metrics_ref.1, f32[4,8,128]{2,1,0:T(8,128)} %inv_ref.1, s32[1,128]{1,0:T(1,128)} %bitcast.1), custom_call_target="tpu_custom_call" | custom-call | flops 60000000 | bytes 500000 | tf_op jit(solution)/shard_map/pallas_call | solution.py:664
  10.0 0.7 %shard_map.60 = (f32[5,4,8,128]{3,2,1,0:T(8,128)}, f32[5,4,8,128]{3,2,1,0:T(8,128)}) custom-call(f32[5,4,8,128]{3,2,1,0:T(8,128)S(1)} %get-tuple-element.4.state_ref, f32[5,4,8,128]{3,2,1,0:T(8,128)S(1)} %get-tuple-element.5.rate_ref), custom_call_target="tpu_custom_call" | custom-call | tf_op jit(solution)/shard_map/pallas_call | solution.py:698
